TPU v7x, 32 devices: a whole 2x2x4 slice. The times are simulated.
32 devices in a mesh: expert: 4 (over x, core), tensor: 8 (over z, y).
Axes of the slice: x: 2, y: 2, z: 4, core: 2. Of those that a mesh axis runs over, the one named last changes fastest.
Arguments:
- tokens: bfloat16 [128, 7168], P('expert', 'tensor'), may hold values from -6 to 6
- routes: int32 [128, 8], P('expert'), may hold values from 0 to 15, all different within a row; in each aligned block of 128 rows (0 to 127, 128 to 255, ...) at most 128 rows name the same one
- gates: bfloat16 [128, 8], P('expert'), may hold values from 0.099609375 to 0.59765625
- w_gate: bfloat16 [16, 2048, 7168], P('expert', 'tensor'), may hold values from -0.0625 to 0.0625
- w_up: bfloat16 [16, 2048, 7168], P('expert', 'tensor'), may hold values from -0.0625 to 0.0625
- w_down: bfloat16 [16, 2048, 7168], P('expert', None, 'tensor'), may hold values from -0.125 to 0.125
Outputs:
- moe_out: bfloat16 [128, 7168], P('expert', 'tensor')
Inputs may be any that keep to these rules, and one draw needn't show every extreme that they name: `routes`: each row names 8 different experts. No expert is named by more than 128 of the 128 rows, and one expert is named by exactly 128 rows.
All inputs are finite; a program needn't handle non-finite values.
Results may differ from a plain program's by a relative error of at most 0.0049.
Values may be sent and summed in bfloat16 or wider, within the bound.
No kernel may reach another device: no remote copies, remote signals or barrier semaphores. Data moves between devices by JAX's collectives and lax.ppermute only.
A program may use at most 128 MiB of HBM per device.

v0:
```python
import jax
import jax.numpy as jnp
from jax import lax
from jax.sharding import PartitionSpec as P

CAP = 128


def entering(value, axis, combine, identity):
    length, index = (lax.axis_size(axis), lax.axis_index(axis))
    everything = lax.all_gather(value, axis)
    start = jnp.broadcast_to(jnp.asarray(identity, value.dtype), value.shape)

    def lap(k, before):
        reached = k < index
        new = combine(before, everything[k])
        return jnp.where(reached, new, before)

    return lax.fori_loop(0, length, lap, start)


def add_counts(earlier, later):
    return earlier + later


def on_device(tokens, routes, gates, w_gate, w_up, w_down):
    exp_dev = w_gate.shape[0]
    experts = exp_dev * lax.axis_size("expert")
    group_index = lax.axis_index("expert")
    expert_ids = jnp.arange(experts, dtype=jnp.int32)
    route_hits = routes[:, :, None] == expert_ids[None, None, :]
    member = jnp.sum(route_hits.astype(jnp.int32), axis=1)
    counts = jnp.sum(member, axis=0)
    offset = entering(counts, "expert", add_counts, jnp.zeros_like(counts))
    before = jnp.cumsum(member, axis=0) - member + offset[None, :]
    own_slot = jnp.sum(jnp.where(route_hits, before[:, None, :], 0), axis=2).astype(jnp.int32)
    all_routes, all_slots = (
        lax.all_gather(routes, "expert", axis=0, tiled=True),
        lax.all_gather(own_slot, "expert", axis=0, tiled=True),
    )
    row_block, all_gates = (
        lax.all_gather(tokens, "expert", axis=0, tiled=True),
        lax.all_gather(gates, "expert", axis=0, tiled=True),
    )
    gathered = lax.all_gather(row_block, "tensor", axis=1, tiled=True)
    local_ids = all_routes - group_index * exp_dev
    is_local = (local_ids >= 0) & (local_ids < exp_dev)
    slot_id = jnp.where(is_local, local_ids * CAP + all_slots, -1)
    slot_range = jnp.arange(exp_dev * CAP, dtype=jnp.int32)
    matches = slot_id[:, :, None] == slot_range[None, None, :]
    picked = jnp.any(matches, axis=1).astype(jnp.bfloat16)
    mixing = jnp.sum(jnp.where(matches, all_gates.astype(jnp.float32)[:, :, None], 0.0), axis=1)
    slot_rows = lax.dot_general(
        picked, gathered, (((0,), (0,)), ((), ())), preferred_element_type=jnp.float32
    ).astype(jnp.bfloat16)
    slot_rows = slot_rows.reshape(exp_dev, CAP, gathered.shape[1])
    gate_proj = jnp.einsum("ecd,efd->ecf", slot_rows, w_gate, preferred_element_type=jnp.float32)
    up_proj = jnp.einsum("ecd,efd->ecf", slot_rows, w_up, preferred_element_type=jnp.float32)
    hidden = (jax.nn.silu(gate_proj) * up_proj).astype(jnp.bfloat16)
    expert_out = jnp.einsum(
        "ecf,efd->ecd",
        lax.all_gather(hidden, "tensor", axis=2, tiled=True),
        w_down,
        preferred_element_type=jnp.float32,
    )
    expert_out = expert_out.reshape(exp_dev * CAP, w_down.shape[2])
    partial_value = jnp.dot(mixing, expert_out, precision=lax.Precision.HIGHEST)
    result = lax.psum_scatter(partial_value, "expert", scatter_dimension=0, tiled=True)
    return result.astype(jnp.bfloat16)


def solution(mesh):
    placed = (
        P("expert", "tensor"),
        P("expert", None),
        P("expert", None),
        P("expert", "tensor", None),
        P("expert", "tensor", None),
        P("expert", None, "tensor"),
    )
    return jax.shard_map(
        on_device, mesh=mesh, in_specs=placed, out_specs=P("expert", "tensor"), check_vma=False
    )
```

profile of v0, /device:TPU:0, one launch (start us, length us, event | category | flops | bytes accessed | tf_op | source)
XLA Modules:
  0.0 181.3 jit_solution(15544654380891682984)
XLA Ops:
  6.5 8.7 %all_gather.29 = bf16[128,896]{1,0:T(8,128)(2,1)} all-gather(bf16[32,896]{1,0:T(8,128)(2,1)} %param.8), channel_id=1, replica_groups=mesh['expert'=4,'tensor'=8] {'expert'}, dimensions={0}, use_global_device_ids=true | all-gather | bytes 286720 | tf_op jit(solution)/shard_map/all_gather | solution.py:42
  15.3 0.0 all-gather.7.cloned.1.call-update
  15.3 0.0 all-gather.9.cloned.1.call-start
  15.3 1.2 dynamic-slice
  17.2 0.8 convert_reduce_fusion
  18.0 0.2 dynamic-update-slice
  18.2 4.3 %all-reduce = s32[64]{0:T(128)S(1)} all-reduce(s32[64]{0:T(128)S(1)} %dynamic-update-slice), channel_id=2, replica_groups=mesh['expert'=4,'tensor'=8] {'expert'}, use_global_device_ids=true, to_apply=%add | all-reduce | flops 64 | bytes 512
  22.5 0.1 reshape.32
  22.6 0.1 copy.18
  22.6 0.1 reduce_window_sum.11
  22.7 0.1 while.14
  22.9 0.1 copy.20
  22.9 0.7 select_reduce_fusion.1
  23.7 5.2 %all-gather.2 = s32[4,32,8]{1,2,0:T(8,128)S(1)} all-gather(s32[1,32,8]{1,2,0:T(8,128)S(1)} %bitcast.29), channel_id=1, replica_groups=mesh['expert'=4,'tensor'=8] {'expert'}, dimensions={0}, use_global_device_ids=true | all-gather | bytes 5120 | tf_op jit(solution)/shard_map/all_gather | solution.py:39
  28.9 5.3 %all-gather.1 = s32[4,32,8]{1,2,0:T(8,128)S(1)} all-gather(s32[1,32,8]{1,2,0:T(8,128)} %bitcast.28), channel_id=1, replica_groups=mesh['expert'=4,'tensor'=8] {'expert'}, dimensions={0}, use_global_device_ids=true | all-gather | bytes 5120 | tf_op jit(solution)/shard_map/all_gather | solution.py:38
  34.2 0.1 copy.25
  34.3 0.7 fusion
  35.0 27.3 %all-gather.7.cloned.1.call-done = bf16[128,7168]{1,0:T(8,128)(2,1)} async-done(((bf16[128,896]{1,0:T(8,128)(2,1)}), bf16[128,7168]{1,0:T(8,128)(2,1)}) %all-gather.7.cloned.1.call-update) | async-done | bytes 1835024 | tf_op jit(solution)/shard_map/all_gather | solution.py:45
  62.3 6.6 %convolution_convert_fusion = bf16[512,7168]{1,0:T(8,128)(2,1)} fusion(pred[128,512]{1,0:T(8,128)(4,1)S(1)} %fusion, bf16[128,7168]{1,0:T(8,128)(2,1)} %all-gather.7.cloned.1.call-done), kind=kOutput, calls=%fused_computation.2 | convolution fusion | flops 943194112 | bytes 9240576 | tf_op jit(solution)/shard_map/dot_general | solution.py:53
  68.9 12.3 %fusion.2 = f32[4,128,256]{2,1,0:T(8,128)S(1)} fusion(bf16[4,128,7168]{2,1,0:T(8,128)(2,1)} %bitcast.22, bf16[4,256,7168]{2,1,0:T(8,128)(2,1)} %param.11), kind=kOutput, calls=%fused_computation.14 | convolution fusion | flops 1879048192 | bytes 22544384 | tf_op jit(solution)/shard_map/ecd,efd->ecf/dot_general | solution.py:57
  81.2 13.0 %fusion.1 = bf16[4,128,256]{2,1,0:T(8,128)(2,1)} fusion(bf16[4,128,7168]{2,1,0:T(8,128)(2,1)} %bitcast.23, bf16[4,256,7168]{2,1,0:T(8,128)(2,1)} %param.12, f32[4,128,256]{2,1,0:T(8,128)S(1)} %fusion.2), kind=kOutput, calls=%fused_computation.7 | convolution fusion | flops 1879834624 | bytes 22806528 | tf_op jit(solution)/shard_map/ecd,efd->ecf/dot_general | solution.py:58
  94.2 0.0 all-gather.9.cloned.1.call-update
  94.2 0.0 reduce-scatter.2.cloned.1.call-start
  94.3 5.4 %all-gather.3 = bf16[4,32,8]{1,2,0:T(8,128)(2,1)S(1)} all-gather(bf16[1,32,8]{1,2,0:T(8,128)(2,1)S(1)} %bitcast.30), channel_id=1, replica_groups=mesh['expert'=4,'tensor'=8] {'expert'}, dimensions={0}, use_global_device_ids=true | all-gather | bytes 2560 | tf_op jit(solution)/shard_map/all_gather | solution.py:43
  99.6 0.1 copy.26
  99.7 0.7 select_reduce_fusion
  100.4 43.1 %all-gather.9.cloned.1.call-done = bf16[4,128,2048]{2,1,0:T(8,128)(2,1)} async-done(((bf16[4,128,256]{2,1,0:T(8,128)(2,1)}), bf16[4,128,2048]{2,1,0:T(8,128)(2,1)}) %all-gather.9.cloned.1.call-update) | async-done | bytes 2097168 | tf_op jit(solution)/shard_map/all_gather | solution.py:62
  143.5 8.2 %fusion.3 = f32[4,128,896]{2,1,0:T(8,128)S(1)} fusion(bf16[4,128,2048]{2,1,0:T(8,128)(2,1)} %all-gather.9.cloned.1.call-done, bf16[4,2048,896]{2,1,0:T(8,128)(2,1)} %param.13), kind=kOutput, calls=%fused_computation.15 | convolution fusion | flops 1879048192 | bytes 18612224 | tf_op jit(solution)/shard_map/ecf,efd->ecd/dot_general | solution.py:60
  151.7 2.0 %fusion.4 = f32[128,896]{1,0:T(8,128)} fusion(f32[128,512]{1,0:T(8,128)S(1)} %select_reduce_fusion, f32[512,896]{1,0:T(8,128)S(1)} %bitcast.24), kind=kOutput, calls=%fused_computation.16 | convolution fusion | flops 704643072 | bytes 2555904 | tf_op jit(solution)/shard_map/dot_general | solution.py:67
  153.7 0.0 reduce-scatter.2.cloned.1.call-update
  153.7 19.5 %reduce-scatter.2.cloned.1.call-done = f32[32,896]{1,0:T(8,128)} async-done(((f32[128,896]{1,0:T(8,128)}), f32[32,896]{1,0:T(8,128)}) %reduce-scatter.2.cloned.1.call-update) | async-done | bytes 114704 | tf_op jit(solution)/shard_map/reduce_scatter | solution.py:68
  173.2 1.5 convert_element_type.20
  (11 shorter events, 0.1 us)
Async XLA Ops:
  6.5 55.8 %all-gather.7.cloned.1.call-start = ((), (), s32[]{:S(2)}) async-start(), calls=%async_computation.1 | async-start | bytes 2064384 | tf_op jit(solution)/shard_map/all_gather | solution.py:45
  15.3 128.3 %all-gather.9.cloned.1.call-start = ((), (), s32[]{:S(2)}) async-start(), calls=%async_computation.2 | async-start | bytes 2359296 | tf_op jit(solution)/shard_map/all_gather | solution.py:62
  81.2 13.1 %copy-start = (bf16[32,8]{0,1:T(8,128)(2,1)S(1)}, bf16[32,8]{0,1:T(8,128)(2,1)}, u32[]{:S(2)}) copy-start(bf16[32,8]{0,1:T(8,128)(2,1)} %param.10) | copy-start | bytes 1540
  94.2 79.0 %reduce-scatter.2.cloned.1.call-start = ((), (), s32[]{:S(2)}) async-start(), calls=%async_computation.3 | async-start | bytes 573440 | tf_op jit(solution)/shard_map/reduce_scatter | solution.py:68
Sparse Core Ops, SparseCore 0:
  15.4 46.8 all-gather.6
  94.3 49.1 all-gather.8
  153.8 19.3 reduce-scatter.1
where the time goes:
time: 182 us; the launch traced here: 181 us
  waiting for transfers between devices  90 us (49%)
  matrix products  42 us (23%)
  blocking collectives  28.9 us (16%)
  between operations  13.8 us (8%)
  other arithmetic  4.59 us (3%)
  local copies, waits for them, and re-layouts  1.88 us (1%)
    all_gather x1, waiting for transfers between devices, on_device(): lax.all_gather(hidden, 'tensor', axis=2, tiled=True)  43.1 us
    all_gather x1, waiting for transfers between devices, on_device(): gathered = lax.all_gather(row_block, 'tensor', axis=1, tiled=True)  27.3 us
    reduce_scatter x1, waiting for transfers between devices, on_device(): lax.psum_scatter(partial_value, 'expert', scatter_dimension=0, tiled=True)  19.5 us
    dot_general x1, matrix products, on_device(): jnp.einsum('ecd,efd->ecf', slot_rows, w_up, preferred_element_type=jnp.fl...  13 us
    dot_general x1, matrix products, on_device(): jnp.einsum('ecd,efd->ecf', slot_rows, w_gate, preferred_element_type=jnp....  12.3 us
    all_gather x1, blocking collectives, on_device(): lax.all_gather(tokens, 'expert', axis=0, tiled=True)  8.71 us
    dot_general x1, matrix products, on_device(): jnp.einsum('ecf,efd->ecd', lax.all_gather(hidden, 'tensor', axis=2, tiled...  8.16 us
    dot_general x1, matrix products, on_device(): lax.dot_general(picked, gathered, (((0,), (0,)), ((), ())), preferred_ele...  6.58 us
  transfers between devices with their start and end apart: 3, of which 3 were waited for; matrix products, arithmetic and copies ran while one was open for 3% of the time, Pallas kernels for 0%

commit v1 on v0

--- a/solution.py
+++ b/solution.py
@@ -1,6 +1,10 @@
+import functools
+
 import jax
 import jax.numpy as jnp
 from jax import lax
+from jax.experimental import pallas as pl
+from jax.experimental.pallas import tpu as pltpu
 from jax.sharding import PartitionSpec as P
 
 CAP = 128
@@ -23,7 +27,7 @@
     return earlier + later
 
 
-def on_device(tokens, routes, gates, w_gate, w_up, w_down):
+def general(tokens, routes, gates, w_gate, w_up, w_down):
     exp_dev = w_gate.shape[0]
     experts = exp_dev * lax.axis_size("expert")
     group_index = lax.axis_index("expert")
@@ -69,6 +73,255 @@
     return result.astype(jnp.bfloat16)
 
 
+COLS = (0, 2, 4, 6, 1, 3, 5, 7)
+ROWS = (0, 2, 1, 3)
+CAPS = (192, 256, 320, 384)
+EARLY = 5
+NT = (((1,), (1,)), ((), ()))
+VMEM = pl.BlockSpec(memory_space=pltpu.VMEM)
+SMEM = pl.BlockSpec(memory_space=pltpu.SMEM)
+HBM = pl.BlockSpec(memory_space=pltpu.HBM)
+
+
+def swap(value, axis, k):
+    n = lax.axis_size(axis)
+    return lax.ppermute(value, axis, [(i, i ^ k) for i in range(n)])
+
+
+def call(body, ins, outs, scratch, limit, *args):
+    return pl.pallas_call(
+        body,
+        in_specs=ins,
+        out_specs=[SMEM if d == jnp.int32 else VMEM for _, d in outs],
+        out_shape=[jax.ShapeDtypeStruct(s, d) if d == jnp.int32 else pltpu.VMEM(s, d) for s, d in outs],
+        scratch_shapes=scratch,
+        compiler_params=pltpu.CompilerParams(vmem_limit_bytes=limit << 20),
+    )(*(a if spec is SMEM else pltpu.with_memory_space_constraint(a, spec.memory_space) for spec, a in zip(ins, args)))
+
+
+def column_copies(at, weights, bufs, sems, blocks, n_e, f_dev, width):
+    made = []
+    for b, (w, buf) in enumerate(zip(weights, bufs)):
+        for e in range(n_e):
+            for j, off in enumerate(blocks):
+                col = pl.multiple_of((at[0] ^ off) * width, 128)
+                src = w.at[e, :, pl.ds(col, width)]
+                dst = buf.at[e * f_dev : (e + 1) * f_dev, j * width : (j + 1) * width]
+                made.append(pltpu.make_async_copy(src, dst, sems.at[b, e, j]))
+    return made
+
+
+def pre_kernel(tokens, routes, gates, out, t_buf, r_buf, g_buf, sems, *, lanes):
+    copies = [
+        pltpu.make_async_copy(src, dst, sems.at[i])
+        for i, (src, dst) in enumerate(((tokens, t_buf), (routes, r_buf), (gates, g_buf)))
+    ]
+    for c in copies:
+        c.start()
+    for c in copies:
+        c.wait()
+    d = tokens.shape[1]
+    out[:, :d] = t_buf[...]
+    ids = lax.broadcasted_iota(jnp.int32, (lanes, tokens.shape[0]), 0)
+    mix = jnp.zeros(ids.shape, jnp.float32)
+    picked, weights = r_buf[...], g_buf[...].astype(jnp.float32)
+    for k in range(picked.shape[0]):
+        mix = mix + jnp.where(picked[k : k + 1] == ids, weights[k : k + 1], 0.0)
+    out[:, d:] = mix.T.astype(out.dtype)
+
+
+def load_kernel(at, wg, wu, g_buf, u_buf, sems, *, n_e, f_dev, width):
+    made = column_copies(at, (wg, wu), (g_buf, u_buf), sems, COLS[:EARLY], n_e, f_dev, width)
+    for c in made:
+        c.start()
+    for c in made:
+        c.wait()
+
+
+def lay(x, mine, other, n, half, width):
+    for j in range(n):
+        x[:half, j * width : (j + 1) * width] = mine[j * half : (j + 1) * half, :]
+        x[half:, j * width : (j + 1) * width] = other[j * half : (j + 1) * half, :]
+
+
+def early_kernel(at, mine, other, g_in, u_in, wg, wu, g_acc, u_acc, mix_t, pos_t, pos_c, taken, g_buf, u_buf, x, m, sems, *, n_e, f_dev, width, half, caps):
+    made = column_copies(at, (wg, wu), (g_buf, u_buf), sems, COLS[EARLY:], n_e, f_dev, width)
+    for c in made:
+        c.start()
+    lay(x, mine, other, EARLY, half, width)
+
+    def one(e, carry):
+        rows = pl.ds(pl.multiple_of(e * f_dev, f_dev), f_dev)
+        g_acc[rows, :] = lax.dot_general(g_in[rows, :], x[...], NT, preferred_element_type=jnp.float32)
+        u_acc[rows, :] = lax.dot_general(u_in[rows, :], x[...], NT, preferred_element_type=jnp.float32)
+        return carry
+
+    lax.fori_loop(0, n_e, one, 0)
+    lanes, rows = m.shape[0], 2 * half
+    mix = jnp.concatenate([r[EARLY * half :, :lanes].astype(jnp.float32) for r in (mine, other)], axis=0)
+    m[...] = mix.T
+    own = m[pl.ds(at[1] * n_e, n_e), :]
+    mix_t[...] = own
+    member = own > 0.0
+    ones = jnp.where(member, 1.0, 0.0)
+    below = lax.broadcasted_iota(jnp.int32, (rows, rows), 0) < lax.broadcasted_iota(jnp.int32, (rows, rows), 1)
+    rank = jnp.dot(ones.astype(jnp.bfloat16), jnp.where(below, 1.0, 0.0).astype(jnp.bfloat16), preferred_element_type=jnp.float32)
+    start = jnp.zeros((1, 1), jnp.float32)
+    m[...] = jnp.full(m.shape, -1.0, jnp.float32)
+    for e in range(n_e):
+        m[e : e + 1, :] = jnp.where(member[e : e + 1], rank[e : e + 1] + start, -1.0)
+        start = start + jnp.sum(ones[e : e + 1], axis=1, keepdims=True)
+    pos_t[...] = m[0:n_e, :]
+    pos_c[...] = m[...].T
+    total, case = start[0, 0], jnp.int32(0)
+    for cap in caps:
+        case = case + jnp.where(total > cap, 1, 0)
+    taken[0] = case
+    for c in made:
+        c.wait()
+
+
+def late_kernel(mine, other, g_in, u_in, g_acc, u_acc, mix_t, pos_t, packed, x, *, n_e, f_dev, width, half):
+    lay(x, mine, other, len(COLS) - EARLY, half, width)
+    slots = lax.broadcasted_iota(jnp.int32, (packed.shape[0], 2 * half), 0).astype(jnp.float32)
+    acc = None
+    for e in range(n_e):
+        rows = slice(e * f_dev, (e + 1) * f_dev)
+        g = g_acc[rows] + lax.dot_general(g_in[rows], x[...], NT, preferred_element_type=jnp.float32)
+        u = u_acc[rows] + lax.dot_general(u_in[rows], x[...], NT, preferred_element_type=jnp.float32)
+        h = (g / (1.0 + jnp.exp(-g)) * u * mix_t[e : e + 1, :]).astype(jnp.bfloat16)
+        pick = jnp.where(slots == pos_t[e : e + 1, :], 1.0, 0.0).astype(jnp.bfloat16)
+        part = lax.dot_general(pick, h, NT, preferred_element_type=jnp.float32)
+        acc = part if acc is None else acc + part
+    packed[...] = acc.astype(jnp.bfloat16)
+
+
+def fetch_kernel(at, wd, d_buf, sems, *, n_e, f_dev):
+    made = []
+    for e in range(n_e):
+        for j, off in enumerate(COLS):
+            row = pl.multiple_of((at[0] ^ off) * f_dev, 128)
+            dst = d_buf.at[e, j * f_dev : (j + 1) * f_dev, :]
+            made.append(pltpu.make_async_copy(wd.at[e, pl.ds(row, f_dev), :], dst, sems.at[e, j]))
+    for c in made:
+        c.start()
+    for c in made:
+        c.wait()
+
+
+def down(blocks, pos_c, wd, n_e, first):
+    f_dev = blocks[0].shape[1]
+    slots = lax.broadcasted_iota(jnp.int32, (pos_c.shape[0], blocks[0].shape[0]), 1).astype(jnp.float32)
+    acc = None
+    for e in range(n_e):
+        place = jnp.where(slots == pos_c[:, e : e + 1], 1.0, 0.0).astype(jnp.bfloat16)
+        h = [jnp.dot(place, b[...], preferred_element_type=jnp.float32).astype(jnp.bfloat16) for b in blocks]
+        units = slice(first * f_dev, (first + len(blocks)) * f_dev)
+        y = jnp.dot(jnp.concatenate(h, axis=1), wd[e, units, :], preferred_element_type=jnp.float32)
+        acc = y if acc is None else acc + y
+    return acc
+
+
+def down_a_kernel(*refs, n_e):
+    blocks, (pos_c, wd, acc) = refs[:EARLY], refs[EARLY:]
+    acc[...] = down(blocks, pos_c, wd, n_e, 0)
+
+
+def down_b_kernel(*refs, n_e):
+    late = len(COLS) - EARLY
+    blocks, (pos_c, wd, acc, own, away) = refs[:late], refs[late:]
+    total = acc[...] + down(blocks, pos_c, wd, n_e, EARLY)
+    n = own.shape[0]
+    own[...] = total[:n]
+    away[...] = total[n:].astype(jnp.bfloat16)
+
+
+def planned(tokens, routes, gates, w_gate, w_up, w_down):
+    n_tok, d_dev = tokens.shape
+    n_e, f_dev, _ = w_gate.shape
+    f_all = w_down.shape[1]
+    half, rows, n = 2 * n_tok, 4 * n_tok, len(COLS)
+    bf16, f32, dma = jnp.bfloat16, jnp.float32, pltpu.SemaphoreType.DMA
+    at = jnp.stack([lax.axis_index("tensor"), lax.axis_index("expert")]).astype(jnp.int32)
+    sizes = dict(n_e=n_e, f_dev=f_dev, width=d_dev)
+
+    (first,) = call(functools.partial(pre_kernel, lanes=128), [HBM] * 3, [((n_tok, d_dev + 128), bf16)],
+        [pltpu.VMEM(tokens.shape, bf16), pltpu.VMEM(routes.T.shape, jnp.int32), pltpu.VMEM(gates.T.shape, bf16), dma((3,))],
+        4, tokens, routes.T, gates.T,
+    )
+    second = swap(first, "expert", 2)
+    both = jnp.concatenate([first, second], axis=0)
+    block, mix2 = both[:, :d_dev], both[:, d_dev:]
+    wide = [((n_e * f_dev, EARLY * d_dev), bf16)] * 2
+    g_a, u_a = call(
+        functools.partial(load_kernel, **sizes), [SMEM, HBM, HBM], wide, [dma((2, n_e, EARLY))], 4, at, w_gate, w_up
+    )
+    y1 = swap(block, "tensor", 1)
+    z2, z4, z6 = (swap(block, "tensor", k) for k in (2, 4, 6))
+    y3, y5, y7 = (swap(z, "tensor", 1) for z in (z2, z4, z6))
+    mix2 = jnp.pad(mix2, ((0, 0), (0, d_dev - 128)))
+    mine_a = jnp.concatenate([block, z2, z4, z6, y1, mix2], axis=0)
+    other_a = swap(mine_a, "expert", 1)
+    late = n - EARLY
+    caps = [c for c in CAPS if c < n_e * rows] + [n_e * rows]
+    g_acc, u_acc, mix_t, pos_t, pos_c, taken, g_b, u_b = call(
+        functools.partial(early_kernel, half=half, caps=caps[:-1], **sizes),
+        [SMEM, VMEM, VMEM, VMEM, VMEM, HBM, HBM],
+        [((n_e * f_dev, rows), f32)] * 2
+        + [((n_e, rows), f32)] * 2
+        + [((rows, 128), f32), ((1,), jnp.int32)]
+        + [((n_e * f_dev, late * d_dev), bf16)] * 2,
+        [pltpu.VMEM((rows, EARLY * d_dev), bf16), pltpu.VMEM((128, rows), f32), dma((2, n_e, late))],
+        8,
+        at, mine_a, other_a, g_a, u_a, w_gate, w_up,
+    )
+    mine_b = jnp.concatenate([y3, y5, y7], axis=0)
+    other_b = swap(mine_b, "expert", 1)
+    (packed,) = call(
+        functools.partial(late_kernel, half=half, **sizes),
+        [VMEM] * 8,
+        [((n_e * rows, f_dev), bf16)],
+        [pltpu.VMEM((rows, late * d_dev), bf16)],
+        8,
+        mine_b, other_b, g_b, u_b, g_acc, u_acc, mix_t, pos_t,
+    )
+
+    def finish(cap, packed, pos_c, w_down, at):
+        hidden = packed[:cap]
+        (wd,) = call(
+            functools.partial(fetch_kernel, n_e=n_e, f_dev=f_dev), [SMEM, HBM], [((n_e, f_all, d_dev), bf16)], [dma((n_e, n))], 4, at, w_down
+        )
+        h1 = swap(hidden, "tensor", 1)
+        h2, h4, h6 = (swap(hidden, "tensor", k) for k in (2, 4, 6))
+        h3, h5, h7 = (swap(h, "tensor", 1) for h in (h2, h4, h6))
+        (acc,) = call(
+            functools.partial(down_a_kernel, n_e=n_e), [VMEM] * (EARLY + 2), [((rows, d_dev), f32)], [], 16,
+            hidden, h2, h4, h6, h1, pos_c, wd,
+        )
+        return call(
+            functools.partial(down_b_kernel, n_e=n_e), [VMEM] * (late + 3),
+            [((n_tok, d_dev), f32), ((3 * n_tok, d_dev), bf16)], [], 16,
+            h3, h5, h7, pos_c, wd, acc,
+        )
+
+    own, away = lax.switch(taken[0], [functools.partial(finish, c) for c in caps], packed, pos_c, w_down, at)
+    total = own
+    for j, k in enumerate(ROWS[1:]):
+        piece = swap(away[j * n_tok : (j + 1) * n_tok], "expert", k)
+        total = total + piece.astype(f32)
+    return total.astype(bf16)
+
+
+def on_device(*args):
+    tokens, _, _, w_gate, _, _ = args
+    n_e, n_t = lax.axis_size("expert"), lax.axis_size("tensor")
+    fits = (n_e, n_t) == (4, 8) and n_e * tokens.shape[0] == CAP
+    tiled = tokens.shape[0] % 16 == 0 and tokens.shape[1] % 128 == 0 and w_gate.shape[1] % 128 == 0
+    if not (fits and tiled):
+        return general(*args)
+    return planned(*args)
+
+
 def solution(mesh):
     placed = (
         P("expert", "tensor"),

time: 182 us -> 81.2 us (0.45)
  waiting for transfers between devices: 90 us -> 20 us
  matrix products: 42 us -> 0 us
  starting transfers between devices: 0.09 us -> 29.7 us
  blocking collectives: 28.9 us -> 0 us
  Pallas kernels: 0 us -> 28.8 us
  between operations: 13.8 us -> 0.79 us
  other arithmetic: 4.59 us -> 0.76 us
    all_gather x2 -> x0, waiting for transfers between devices: 70.4 us -> none  [the longest x1 43.1 us: on_device(): lax.all_gather(hidden, 'tensor', axis=2, tiled=True)]
    dot_general x5 -> x0, matrix products: 42 us -> none  [the longest x1 13 us: on_device(): jnp.einsum('ecd,efd->ecf', slot_rows, w_up, preferred_element_type=jnp.fl...]
    ppermute x0 -> x20, starting transfers between devices: none -> 29.7 us  [swap(): return lax.ppermute(value, axis, [(i, i ^ k) for i in range(n)])]
    pallas_call x0 -> x7, Pallas kernels: none -> 28.8 us  [call(): pl.pallas_call(body, in_specs=ins, out_specs=[SMEM if d == jnp.int32 else...]
    all_gather x4 -> x0, blocking collectives: 24.6 us -> none  [the longest x1 8.71 us: on_device(): lax.all_gather(tokens, 'expert', axis=0, tiled=True)]
    ppermute x0 -> x20, waiting for transfers between devices: none -> 20 us  [swap(): return lax.ppermute(value, axis, [(i, i ^ k) for i in range(n)])]
    reduce_scatter x1 -> x0, waiting for transfers between devices: 19.5 us -> none  [on_device(): lax.psum_scatter(partial_value, 'expert', scatter_dimension=0, tiled=True)]
    unnamed x1 -> x0, blocking collectives: 4.26 us -> none
  transfers between devices with their start and end apart: 3 -> 20, of which waited for: 3 -> 8; matrix products, arithmetic and copies ran while one was open for 3% -> 0% of each run, Pallas kernels for 0% -> 28%
where the time goes in v1:
time: 81.2 us; the launch traced here: 81 us
  starting transfers between devices  29.7 us (37%)
  Pallas kernels  28.8 us (35%)
  waiting for transfers between devices  20 us (25%)
    ppermute x20, starting transfers between devices, swap(): return lax.ppermute(value, axis, [(i, i ^ k) for i in range(n)])  29.7 us
    pallas_call x7, Pallas kernels, call(): pl.pallas_call(body, in_specs=ins, out_specs=[SMEM if d == jnp.int32 else...  28.8 us
    ppermute x20, waiting for transfers between devices, swap(): return lax.ppermute(value, axis, [(i, i ^ k) for i in range(n)])  20 us
  transfers between devices with their start and end apart: 20, of which 8 were waited for; matrix products, arithmetic and copies ran while one was open for 0% of the time, Pallas kernels for 28%

profile of v1, /device:TPU:0, one launch (start us, length us, event | category | flops | bytes accessed | tf_op | source)
XLA Modules:
  0.0 81.0 jit_solution(17978217869312489303)
XLA Ops:
  0.0 1.0 %shard_map.64 = bf16[32,1024]{1,0:T(8,128)(2,1)S(1)} custom-call(bf16[32,896]{1,0:T(8,128)(2,1)} %tokens.1, s32[8,32]{1,0:T(8,128)} %bitcast.5, bf16[8,32]{1,0:T(8,128)(2,1)} %bitcast.6), custom_call_target="tpu_custom_call" | custom-call | tf_op jit(solution)/shard_map/pallas_call | solution.py:92
  1.0 3.0 %collective-permute-start.35 = (bf16[32,1024]{1,0:T(8,128)(2,1)S(1)}, bf16[32,1024]{1,0:T(8,128)(2,1)S(1)}, u32[]{:S(2)}, u32[]{:S(2)}) collective-permute-start(bf16[32,1024]{1,0:T(8,128)(2,1)S(1)} %shard_map.64), channel_id=1, source_target_pairs={{0,16},{8,24},{16,0},{24,8},{1,17},{9,25},{17,1},{25,9},{2,18},{10... | collective-permute-start | bytes 196616 | tf_op jit(solution)/shard_map/ppermute | solution.py:88
  4.0 2.2 %collective-permute-done.35 = bf16[32,1024]{1,0:T(8,128)(2,1)S(1)} collective-permute-done((bf16[32,1024]{1,0:T(8,128)(2,1)S(1)}, bf16[32,1024]{1,0:T(8,128)(2,1)S(1)}, u32[]{:S(2)}, u32[]{:S(2)}) %collective-permute-start.35) | collective-permute-done | bytes 65568 | tf_op jit(solution)/shard_map/ppermute | solution.py:88
  6.3 2.2 %collective-permute-start.36 = (bf16[64,896]{1,0:T(8,128)(2,1)S(1)}, bf16[64,896]{1,0:T(8,128)(2,1)S(1)}, u32[]{:S(2)}, u32[]{:S(2)}) collective-permute-start(bf16[64,896]{1,0:T(8,128)(2,1)S(1)} %get-tuple-element.90), channel_id=1, source_target_pairs={{0,2},{1,3},{2,0},{3,1},{4,6},{5,7},{6,4},{7,5},{8,10},{9,11},{10,... | collective-permute-start | bytes 344072 | tf_op jit(solution)/shard_map/ppermute | solution.py:88
  8.4 2.6 %collective-permute-start.37 = (bf16[64,896]{1,0:T(8,128)(2,1)S(1)}, bf16[64,896]{1,0:T(8,128)(2,1)S(1)}, u32[]{:S(2)}, u32[]{:S(2)}) collective-permute-start(bf16[64,896]{1,0:T(8,128)(2,1)S(1)} %get-tuple-element.90), channel_id=1, source_target_pairs={{0,4},{1,5},{2,6},{3,7},{4,0},{5,1},{6,2},{7,3},{8,12},{9,13},{10,... | collective-permute-start | bytes 344072 | tf_op jit(solution)/shard_map/ppermute | solution.py:88
  11.0 1.7 %collective-permute-start.39 = (bf16[64,896]{1,0:T(8,128)(2,1)S(1)}, bf16[64,896]{1,0:T(8,128)(2,1)S(1)}, u32[]{:S(2)}, u32[]{:S(2)}) collective-permute-start(bf16[64,896]{1,0:T(8,128)(2,1)S(1)} %get-tuple-element.90), channel_id=1, source_target_pairs={{0,1},{1,0},{2,3},{3,2},{4,5},{5,4},{6,7},{7,6},{8,9},{9,8},{10,11... | collective-permute-start | bytes 344072 | tf_op jit(solution)/shard_map/ppermute | solution.py:88
  12.8 1.5 %collective-permute-start.41 = (bf16[64,896]{1,0:T(8,128)(2,1)S(1)}, bf16[64,896]{1,0:T(8,128)(2,1)S(1)}, u32[]{:S(2)}, u32[]{:S(2)}) collective-permute-start(bf16[64,896]{1,0:T(8,128)(2,1)S(1)} %collective-permute-done.36), channel_id=1, source_target_pairs={{0,1},{1,0},{2,3},{3,2},{4,5},{5,4},{6,7},{7,6},{8,9},{9,8},{10,11... | collective-permute-start | bytes 344072 | tf_op jit(solution)/shard_map/ppermute | solution.py:88
  14.3 4.7 %collective-permute-done.37 = bf16[64,896]{1,0:T(8,128)(2,1)S(1)} collective-permute-done((bf16[64,896]{1,0:T(8,128)(2,1)S(1)}, bf16[64,896]{1,0:T(8,128)(2,1)S(1)}, u32[]{:S(2)}, u32[]{:S(2)}) %collective-permute-start.37) | collective-permute-done | bytes 114720 | tf_op jit(solution)/shard_map/ppermute | solution.py:88
  19.2 1.5 %collective-permute-start.42 = (bf16[64,896]{1,0:T(8,128)(2,1)S(1)}, bf16[64,896]{1,0:T(8,128)(2,1)S(1)}, u32[]{:S(2)}, u32[]{:S(2)}) collective-permute-start(bf16[64,896]{1,0:T(8,128)(2,1)S(1)} %collective-permute-done.37), channel_id=1, source_target_pairs={{0,1},{1,0},{2,3},{3,2},{4,5},{5,4},{6,7},{7,6},{8,9},{9,8},{10,11... | collective-permute-start | bytes 344072 | tf_op jit(solution)/shard_map/ppermute | solution.py:88
  20.7 0.6 collective-permute-start.43
  21.3 4.0 %collective-permute-done.42 = bf16[64,896]{1,0:T(8,128)(2,1)S(1)} collective-permute-done((bf16[64,896]{1,0:T(8,128)(2,1)S(1)}, bf16[64,896]{1,0:T(8,128)(2,1)S(1)}, u32[]{:S(2)}, u32[]{:S(2)}) %collective-permute-start.42) | collective-permute-done | bytes 114720 | tf_op jit(solution)/shard_map/ppermute | solution.py:88
  25.3 1.9 %collective-permute-done.43 = bf16[64,896]{1,0:T(8,128)(2,1)S(1)} collective-permute-done((bf16[64,896]{1,0:T(8,128)(2,1)S(1)}, bf16[64,896]{1,0:T(8,128)(2,1)S(1)}, u32[]{:S(2)}, u32[]{:S(2)}) %collective-permute-start.43) | collective-permute-done | bytes 114720 | tf_op jit(solution)/shard_map/ppermute | solution.py:88
  27.3 7.2 %shard_map.65 = (bf16[1024,4480]{1,0:T(8,128)(2,1)S(1)}, bf16[1024,4480]{1,0:T(8,128)(2,1)S(1)}) custom-call(s32[2]{0:T(128)S(1)} %pad_add_fusion.at, bf16[4,256,7168]{2,1,0:T(8,128)(2,1)} %wg.3, bf16[4,256,7168]{2,1,0:T(8,128)(2,1)} %wu.3), custom_call_target="tpu_custom_call" | custom-call | tf_op jit(solution)/shard_map/pallas_call | solution.py:92
  34.5 7.1 %shard_map.66 = (f32[1024,128]{1,0:T(8,128)S(1)}, f32[1024,128]{1,0:T(8,128)S(1)}, f32[4,128]{1,0:T(4,128)S(1)}, f32[4,128]{1,0:T(4,128)S(1)}, f32[128,128]{1,0:...) custom-call(s32[2]{0:T(128)S(1)} %pad_add_fusion.at, ...), custom_call_target="tpu_custom_call" | custom-call | tf_op jit(solution)/shard_map/pallas_call | solution.py:92
  41.7 4.0 %shard_map.67 = bf16[512,256]{1,0:T(8,128)(2,1)S(1)} custom-call(bf16[192,896]{1,0:T(8,128)(2,1)S(1)} %constant_dynamic-update-slice_fusion.5.mine, bf16[192,896]{1,0:T(8,128)(2,1)S(1)} %collective-permute-done.44.other, bf16[1024,2688]{1,0:T(8,128)(2,1)S(1)} %get-tuple-element.80.g_in, bf16[1024,2688]{1,0:T(8,128)(2,1)S(1)} %get-tuple-element.81.u_in, ...), custom_call_target="tpu_custom_call" | custom-call | tf_op jit(solution)/shard_map/pallas_call | solution.py:92
  46.3 24.5 %conditional.1 = ((f32[32,896]{1,0:T(8,128)S(1)}, bf16[96,896]{1,0:T(8,128)(2,1)S(1)})) conditional(s32[]{:T(128)} %bitcast.4, (bf16[512,256]{1,0:T(8,128)(2,1)S(1)}, s32[2]{0:T(128)S(1)}, bf16[4,2048,896]{2,1,0:T(8,128)(2,1)}, f32[128,128]{1,0:T(8,128)S(1)}) %tuple.20, (bf16[512,256]{1,0:T(8,128)(2,1)S(1)}, ...), branch_computations={%region_0.1_spmd, %region_1.2_spmd, %region_2.3_spmd, %region_3.4_... | conditional | bytes 7340320 | solution.py:307
  46.5 2.8 %collective-permute-start.9 = (bf16[256,256]{1,0:T(8,128)(2,1)S(1)}, bf16[256,256]{1,0:T(8,128)(2,1)S(1)}, u32[]{:S(2)}, u32[]{:S(2)}) collective-permute-start(bf16[256,256]{1,0:T(8,128)(2,1)S(1)} %slice.19.refs_0_), channel_id=1, source_target_pairs={{0,4},{1,5},{2,6},{3,7},{4,0},{5,1},{6,2},{7,3},{8,12},{9,13},{10,... | collective-permute-start | bytes 393224 | tf_op jit(solution)/shard_map/cond/branch_1_fun/ppermute | solution.py:88
  49.4 1.5 %collective-permute-start.11 = (bf16[256,256]{1,0:T(8,128)(2,1)S(1)}, bf16[256,256]{1,0:T(8,128)(2,1)S(1)}, u32[]{:S(2)}, u32[]{:S(2)}) collective-permute-start(bf16[256,256]{1,0:T(8,128)(2,1)S(1)} %slice.19.refs_0_), channel_id=1, source_target_pairs={{0,6},{1,7},{2,4},{3,5},{4,2},{5,3},{6,0},{7,1},{8,14},{9,15},{10,... | collective-permute-start | bytes 393224 | tf_op jit(solution)/shard_map/cond/branch_1_fun/ppermute | solution.py:88
  50.9 1.4 %collective-permute-start.13 = (bf16[256,256]{1,0:T(8,128)(2,1)S(1)}, bf16[256,256]{1,0:T(8,128)(2,1)S(1)}, u32[]{:S(2)}, u32[]{:S(2)}) collective-permute-start(bf16[256,256]{1,0:T(8,128)(2,1)S(1)} %slice.19.refs_0_), channel_id=1, source_target_pairs={{0,1},{1,0},{2,3},{3,2},{4,5},{5,4},{6,7},{7,6},{8,9},{9,8},{10,11... | collective-permute-start | bytes 393224 | tf_op jit(solution)/shard_map/cond/branch_1_fun/ppermute | solution.py:88
  52.2 1.1 %collective-permute-done.9.refs_2_ = bf16[256,256]{1,0:T(8,128)(2,1)S(1)} collective-permute-done((bf16[256,256]{1,0:T(8,128)(2,1)S(1)}, bf16[256,256]{1,0:T(8,128)(2,1)S(1)}, u32[]{:S(2)}, u32[]{:S(2)}) %collective-permute-start.9) | collective-permute-done | bytes 131104 | tf_op jit(solution)/shard_map/cond/branch_1_fun/ppermute | solution.py:88
  53.3 2.1 %collective-permute-start.10 = (bf16[256,256]{1,0:T(8,128)(2,1)S(1)}, bf16[256,256]{1,0:T(8,128)(2,1)S(1)}, u32[]{:S(2)}, u32[]{:S(2)}) collective-permute-start(bf16[256,256]{1,0:T(8,128)(2,1)S(1)} %collective-permute-done.9.refs_2_), channel_id=1, source_target_pairs={{0,1},{1,0},{2,3},{3,2},{4,5},{5,4},{6,7},{7,6},{8,9},{9,8},{10,11... | collective-permute-start | bytes 393224 | tf_op jit(solution)/shard_map/cond/branch_1_fun/ppermute | solution.py:88
  55.4 2.7 %collective-permute-done.11.refs_3_ = bf16[256,256]{1,0:T(8,128)(2,1)S(1)} collective-permute-done((bf16[256,256]{1,0:T(8,128)(2,1)S(1)}, bf16[256,256]{1,0:T(8,128)(2,1)S(1)}, u32[]{:S(2)}, u32[]{:S(2)}) %collective-permute-start.11) | collective-permute-done | bytes 131104 | tf_op jit(solution)/shard_map/cond/branch_1_fun/ppermute | solution.py:88
  58.1 1.3 %collective-permute-start.12 = (bf16[256,256]{1,0:T(8,128)(2,1)S(1)}, bf16[256,256]{1,0:T(8,128)(2,1)S(1)}, u32[]{:S(2)}, u32[]{:S(2)}) collective-permute-start(bf16[256,256]{1,0:T(8,128)(2,1)S(1)} %collective-permute-done.11.refs_3_), channel_id=1, source_target_pairs={{0,1},{1,0},{2,3},{3,2},{4,5},{5,4},{6,7},{7,6},{8,9},{9,8},{10,11... | collective-permute-start | bytes 393224 | tf_op jit(solution)/shard_map/cond/branch_1_fun/ppermute | solution.py:88
  59.5 1.2 %collective-permute-start.8 = (bf16[256,256]{1,0:T(8,128)(2,1)S(1)}, bf16[256,256]{1,0:T(8,128)(2,1)S(1)}, u32[]{:S(2)}, u32[]{:S(2)}) collective-permute-start(bf16[256,256]{1,0:T(8,128)(2,1)S(1)} %collective-permute-done.7.refs_1_), channel_id=1, source_target_pairs={{0,1},{1,0},{2,3},{3,2},{4,5},{5,4},{6,7},{7,6},{8,9},{9,8},{10,11... | collective-permute-start | bytes 393224 | tf_op jit(solution)/shard_map/cond/branch_1_fun/ppermute | solution.py:88
  60.6 6.0 %branch_1_fun.3.refs_6_.refs_4_ = bf16[4,2048,896]{2,1,0:T(8,128)(2,1)S(1)} custom-call(s32[2]{0:T(128)S(1)} %get-tuple-element.51.at, bf16[4,2048,896]{2,1,0:T(8,128)(2,1)} %get-tuple-element.52.wd), custom_call_target="tpu_custom_call" | custom-call | tf_op jit(solution)/shard_map/cond/branch_1_fun/pallas_call | solution.py:92
  66.6 2.1 %branch_1_fun.4.refs_5_ = f32[128,896]{1,0:T(8,128)S(1)} custom-call(bf16[256,256]{1,0:T(8,128)(2,1)S(1)} %slice.19.refs_0_, bf16[256,256]{1,0:T(8,128)(2,1)S(1)} %collective-permute-done.7.refs_1_, bf16[256,256]{1,0:T(8,128)(2,1)S(1)} %collective-permute-done.9.refs_2_, bf16[256,256]{1,0:T(8,128)(2,1)S(1)} %collective-permute-done.11.refs_3_, ...), custom_call_target="tpu_custom_call" | custom-call | tf_op jit(solution)/shard_map/cond/branch_1_fun/pallas_call | solution.py:92
  68.8 1.5 %branch_1_fun.5 = (f32[32,896]{1,0:T(8,128)S(1)}, bf16[96,896]{1,0:T(8,128)(2,1)S(1)}) custom-call(bf16[256,256]{1,0:T(8,128)(2,1)S(1)} %collective-permute-done.8.refs_0_, bf16[256,256]{1,0:T(8,128)(2,1)S(1)} %collective-permute-done.10.refs_1_, bf16[256,256]{1,0:T(8,128)(2,1)S(1)} %collective-permute-done.12.refs_2_, ...), custom_call_target="tpu_custom_call" | custom-call | tf_op jit(solution)/shard_map/cond/branch_1_fun/pallas_call | solution.py:92
  70.8 5.9 %collective-permute-start.45 = (bf16[32,896]{1,0:T(8,128)(2,1)S(1)}, bf16[32,896]{1,0:T(8,128)(2,1)S(1)}, u32[]{:S(2)}, u32[]{:S(2)}) collective-permute-start(bf16[32,896]{1,0:T(8,128)(2,1)S(1)} %get-tuple-element.91), channel_id=1, source_target_pairs={{0,16},{8,24},{16,0},{24,8},{1,17},{9,25},{17,1},{25,9},{2,18},{10... | collective-permute-start | bytes 172040 | tf_op jit(solution)/shard_map/ppermute | solution.py:88
  76.7 0.2 collective-permute-start.47
  76.9 2.0 %collective-permute-done.45 = bf16[32,896]{1,0:T(8,128)(2,1)S(1)} collective-permute-done((bf16[32,896]{1,0:T(8,128)(2,1)S(1)}, bf16[32,896]{1,0:T(8,128)(2,1)S(1)}, u32[]{:S(2)}, u32[]{:S(2)}) %collective-permute-start.45) | collective-permute-done | bytes 57376 | tf_op jit(solution)/shard_map/ppermute | solution.py:88
  78.9 1.4 %collective-permute-done.47 = bf16[32,896]{1,0:T(8,128)(2,1)S(1)} collective-permute-done((bf16[32,896]{1,0:T(8,128)(2,1)S(1)}, bf16[32,896]{1,0:T(8,128)(2,1)S(1)}, u32[]{:S(2)}, u32[]{:S(2)}) %collective-permute-start.47) | collective-permute-done | bytes 57376 | tf_op jit(solution)/shard_map/ppermute | solution.py:88
  80.3 0.7 add_convert_fusion
  (29 shorter events, 0.4 us)
Async XLA Ops:
  1.0 5.3 %collective-permute-start.35 = (bf16[32,1024]{1,0:T(8,128)(2,1)S(1)}, bf16[32,1024]{1,0:T(8,128)(2,1)S(1)}, u32[]{:S(2)}, u32[]{:S(2)}) collective-permute-start(bf16[32,1024]{1,0:T(8,128)(2,1)S(1)} %shard_map.64), channel_id=1, source_target_pairs={{0,16},{8,24},{16,0},{24,8},{1,17},{9,25},{17,1},{25,9},{2,18},{10... | collective-permute-start | bytes 196616 | tf_op jit(solution)/shard_map/ppermute | solution.py:88
  6.3 6.5 %collective-permute-start.36 = (bf16[64,896]{1,0:T(8,128)(2,1)S(1)}, bf16[64,896]{1,0:T(8,128)(2,1)S(1)}, u32[]{:S(2)}, u32[]{:S(2)}) collective-permute-start(bf16[64,896]{1,0:T(8,128)(2,1)S(1)} %get-tuple-element.90), channel_id=1, source_target_pairs={{0,2},{1,3},{2,0},{3,1},{4,6},{5,7},{6,4},{7,5},{8,10},{9,11},{10,... | collective-permute-start | bytes 344072 | tf_op jit(solution)/shard_map/ppermute | solution.py:88
  8.4 10.5 %collective-permute-start.37 = (bf16[64,896]{1,0:T(8,128)(2,1)S(1)}, bf16[64,896]{1,0:T(8,128)(2,1)S(1)}, u32[]{:S(2)}, u32[]{:S(2)}) collective-permute-start(bf16[64,896]{1,0:T(8,128)(2,1)S(1)} %get-tuple-element.90), channel_id=1, source_target_pairs={{0,4},{1,5},{2,6},{3,7},{4,0},{5,1},{6,2},{7,3},{8,12},{9,13},{10,... | collective-permute-start | bytes 344072 | tf_op jit(solution)/shard_map/ppermute | solution.py:88
  11.0 8.0 %collective-permute-start.38 = (bf16[64,896]{1,0:T(8,128)(2,1)S(1)}, bf16[64,896]{1,0:T(8,128)(2,1)S(1)}, u32[]{:S(2)}, u32[]{:S(2)}) collective-permute-start(bf16[64,896]{1,0:T(8,128)(2,1)S(1)} %get-tuple-element.90), channel_id=1, source_target_pairs={{0,6},{1,7},{2,4},{3,5},{4,2},{5,3},{6,0},{7,1},{8,14},{9,15},{10,... | collective-permute-start | bytes 344072 | tf_op jit(solution)/shard_map/ppermute | solution.py:88
  11.0 8.0 %collective-permute-start.39 = (bf16[64,896]{1,0:T(8,128)(2,1)S(1)}, bf16[64,896]{1,0:T(8,128)(2,1)S(1)}, u32[]{:S(2)}, u32[]{:S(2)}) collective-permute-start(bf16[64,896]{1,0:T(8,128)(2,1)S(1)} %get-tuple-element.90), channel_id=1, source_target_pairs={{0,1},{1,0},{2,3},{3,2},{4,5},{5,4},{6,7},{7,6},{8,9},{9,8},{10,11... | collective-permute-start | bytes 344072 | tf_op jit(solution)/shard_map/ppermute | solution.py:88
  12.8 8.5 %collective-permute-start.41 = (bf16[64,896]{1,0:T(8,128)(2,1)S(1)}, bf16[64,896]{1,0:T(8,128)(2,1)S(1)}, u32[]{:S(2)}, u32[]{:S(2)}) collective-permute-start(bf16[64,896]{1,0:T(8,128)(2,1)S(1)} %collective-permute-done.36), channel_id=1, source_target_pairs={{0,1},{1,0},{2,3},{3,2},{4,5},{5,4},{6,7},{7,6},{8,9},{9,8},{10,11... | collective-permute-start | bytes 344072 | tf_op jit(solution)/shard_map/ppermute | solution.py:88
  19.1 15.5 %collective-permute-start.40 = (bf16[384,896]{1,0:T(8,128)(2,1)S(1)}, bf16[384,896]{1,0:T(8,128)(2,1)S(1)}, u32[]{:S(2)}, u32[]{:S(2)}) collective-permute-start(bf16[384,896]{1,0:T(8,128)(2,1)S(1)} %fusion.4.mine), channel_id=1, source_target_pairs={{0,8},{8,0},{16,24},{24,16},{1,9},{9,1},{17,25},{25,17},{2,10},{10... | collective-permute-start | bytes 2064392 | tf_op jit(solution)/shard_map/ppermute | solution.py:88
  19.2 6.1 %collective-permute-start.42 = (bf16[64,896]{1,0:T(8,128)(2,1)S(1)}, bf16[64,896]{1,0:T(8,128)(2,1)S(1)}, u32[]{:S(2)}, u32[]{:S(2)}) collective-permute-start(bf16[64,896]{1,0:T(8,128)(2,1)S(1)} %collective-permute-done.37), channel_id=1, source_target_pairs={{0,1},{1,0},{2,3},{3,2},{4,5},{5,4},{6,7},{7,6},{8,9},{9,8},{10,11... | collective-permute-start | bytes 344072 | tf_op jit(solution)/shard_map/ppermute | solution.py:88
  20.7 6.5 %collective-permute-start.43 = (bf16[64,896]{1,0:T(8,128)(2,1)S(1)}, bf16[64,896]{1,0:T(8,128)(2,1)S(1)}, u32[]{:S(2)}, u32[]{:S(2)}) collective-permute-start(bf16[64,896]{1,0:T(8,128)(2,1)S(1)} %collective-permute-done.38), channel_id=1, source_target_pairs={{0,1},{1,0},{2,3},{3,2},{4,5},{5,4},{6,7},{7,6},{8,9},{9,8},{10,11... | collective-permute-start | bytes 344072 | tf_op jit(solution)/shard_map/ppermute | solution.py:88
  27.2 14.5 %collective-permute-start.44 = (bf16[192,896]{1,0:T(8,128)(2,1)S(1)}, bf16[192,896]{1,0:T(8,128)(2,1)S(1)}, u32[]{:S(2)}, u32[]{:S(2)}) collective-permute-start(bf16[192,896]{1,0:T(8,128)(2,1)S(1)} %constant_dynamic-update-slice_fusion.5.mine), channel_id=1, source_target_pairs={{0,8},{8,0},{16,24},{24,16},{1,9},{9,1},{17,25},{25,17},{2,10},{10... | collective-permute-start | bytes 1032200 | tf_op jit(solution)/shard_map/ppermute | solution.py:88
  46.5 6.8 %collective-permute-start.9 = (bf16[256,256]{1,0:T(8,128)(2,1)S(1)}, bf16[256,256]{1,0:T(8,128)(2,1)S(1)}, u32[]{:S(2)}, u32[]{:S(2)}) collective-permute-start(bf16[256,256]{1,0:T(8,128)(2,1)S(1)} %slice.19.refs_0_), channel_id=1, source_target_pairs={{0,4},{1,5},{2,6},{3,7},{4,0},{5,1},{6,2},{7,3},{8,12},{9,13},{10,... | collective-permute-start | bytes 393224 | tf_op jit(solution)/shard_map/cond/branch_1_fun/ppermute | solution.py:88
  49.4 8.7 %collective-permute-start.11 = (bf16[256,256]{1,0:T(8,128)(2,1)S(1)}, bf16[256,256]{1,0:T(8,128)(2,1)S(1)}, u32[]{:S(2)}, u32[]{:S(2)}) collective-permute-start(bf16[256,256]{1,0:T(8,128)(2,1)S(1)} %slice.19.refs_0_), channel_id=1, source_target_pairs={{0,6},{1,7},{2,4},{3,5},{4,2},{5,3},{6,0},{7,1},{8,14},{9,15},{10,... | collective-permute-start | bytes 393224 | tf_op jit(solution)/shard_map/cond/branch_1_fun/ppermute | solution.py:88
  50.9 8.6 %collective-permute-start.7 = (bf16[256,256]{1,0:T(8,128)(2,1)S(1)}, bf16[256,256]{1,0:T(8,128)(2,1)S(1)}, u32[]{:S(2)}, u32[]{:S(2)}) collective-permute-start(bf16[256,256]{1,0:T(8,128)(2,1)S(1)} %slice.19.refs_0_), channel_id=1, source_target_pairs={{0,2},{1,3},{2,0},{3,1},{4,6},{5,7},{6,4},{7,5},{8,10},{9,11},{10,... | collective-permute-start | bytes 393224 | tf_op jit(solution)/shard_map/cond/branch_1_fun/ppermute | solution.py:88
  50.9 15.8 %collective-permute-start.13 = (bf16[256,256]{1,0:T(8,128)(2,1)S(1)}, bf16[256,256]{1,0:T(8,128)(2,1)S(1)}, u32[]{:S(2)}, u32[]{:S(2)}) collective-permute-start(bf16[256,256]{1,0:T(8,128)(2,1)S(1)} %slice.19.refs_0_), channel_id=1, source_target_pairs={{0,1},{1,0},{2,3},{3,2},{4,5},{5,4},{6,7},{7,6},{8,9},{9,8},{10,11... | collective-permute-start | bytes 393224 | tf_op jit(solution)/shard_map/cond/branch_1_fun/ppermute | solution.py:88
  53.3 15.4 %collective-permute-start.10 = (bf16[256,256]{1,0:T(8,128)(2,1)S(1)}, bf16[256,256]{1,0:T(8,128)(2,1)S(1)}, u32[]{:S(2)}, u32[]{:S(2)}) collective-permute-start(bf16[256,256]{1,0:T(8,128)(2,1)S(1)} %collective-permute-done.9.refs_2_), channel_id=1, source_target_pairs={{0,1},{1,0},{2,3},{3,2},{4,5},{5,4},{6,7},{7,6},{8,9},{9,8},{10,11... | collective-permute-start | bytes 393224 | tf_op jit(solution)/shard_map/cond/branch_1_fun/ppermute | solution.py:88
  58.1 10.6 %collective-permute-start.12 = (bf16[256,256]{1,0:T(8,128)(2,1)S(1)}, bf16[256,256]{1,0:T(8,128)(2,1)S(1)}, u32[]{:S(2)}, u32[]{:S(2)}) collective-permute-start(bf16[256,256]{1,0:T(8,128)(2,1)S(1)} %collective-permute-done.11.refs_3_), channel_id=1, source_target_pairs={{0,1},{1,0},{2,3},{3,2},{4,5},{5,4},{6,7},{7,6},{8,9},{9,8},{10,11... | collective-permute-start | bytes 393224 | tf_op jit(solution)/shard_map/cond/branch_1_fun/ppermute | solution.py:88
  59.5 9.3 %collective-permute-start.8 = (bf16[256,256]{1,0:T(8,128)(2,1)S(1)}, bf16[256,256]{1,0:T(8,128)(2,1)S(1)}, u32[]{:S(2)}, u32[]{:S(2)}) collective-permute-start(bf16[256,256]{1,0:T(8,128)(2,1)S(1)} %collective-permute-done.7.refs_1_), channel_id=1, source_target_pairs={{0,1},{1,0},{2,3},{3,2},{4,5},{5,4},{6,7},{7,6},{8,9},{9,8},{10,11... | collective-permute-start | bytes 393224 | tf_op jit(solution)/shard_map/cond/branch_1_fun/ppermute | solution.py:88
  70.8 8.1 %collective-permute-start.45 = (bf16[32,896]{1,0:T(8,128)(2,1)S(1)}, bf16[32,896]{1,0:T(8,128)(2,1)S(1)}, u32[]{:S(2)}, u32[]{:S(2)}) collective-permute-start(bf16[32,896]{1,0:T(8,128)(2,1)S(1)} %get-tuple-element.91), channel_id=1, source_target_pairs={{0,16},{8,24},{16,0},{24,8},{1,17},{9,25},{17,1},{25,9},{2,18},{10... | collective-permute-start | bytes 172040 | tf_op jit(solution)/shard_map/ppermute | solution.py:88
  76.7 2.2 %collective-permute-start.46 = (bf16[32,896]{1,0:T(8,128)(2,1)S(1)}, bf16[32,896]{1,0:T(8,128)(2,1)S(1)}, u32[]{:S(2)}, u32[]{:S(2)}) collective-permute-start(bf16[32,896]{1,0:T(8,128)(2,1)S(1)} %get-tuple-element.93), channel_id=1, source_target_pairs={{0,8},{8,0},{16,24},{24,16},{1,9},{9,1},{17,25},{25,17},{2,10},{10... | collective-permute-start | bytes 172040 | tf_op jit(solution)/shard_map/ppermute | solution.py:88
  76.7 3.6 %collective-permute-start.47 = (bf16[32,896]{1,0:T(8,128)(2,1)S(1)}, bf16[32,896]{1,0:T(8,128)(2,1)S(1)}, u32[]{:S(2)}, u32[]{:S(2)}) collective-permute-start(bf16[32,896]{1,0:T(8,128)(2,1)S(1)} %get-tuple-element.92), channel_id=1, source_target_pairs={{0,24},{8,16},{16,8},{24,0},{1,25},{9,17},{17,9},{25,1},{2,26},{10... | collective-permute-start | bytes 172040 | tf_op jit(solution)/shard_map/ppermute | solution.py:88

commit v2 on v0

--- a/solution.py
+++ b/solution.py
@@ -1,6 +1,10 @@
+import functools
+
 import jax
 import jax.numpy as jnp
 from jax import lax
+from jax.experimental import pallas as pl
+from jax.experimental.pallas import tpu as pltpu
 from jax.sharding import PartitionSpec as P
 
 CAP = 128
@@ -23,7 +27,7 @@
     return earlier + later
 
 
-def on_device(tokens, routes, gates, w_gate, w_up, w_down):
+def general(tokens, routes, gates, w_gate, w_up, w_down):
     exp_dev = w_gate.shape[0]
     experts = exp_dev * lax.axis_size("expert")
     group_index = lax.axis_index("expert")
@@ -69,6 +73,309 @@
     return result.astype(jnp.bfloat16)
 
 
+COLS = (0, 1, 2, 4, 3, 5, 6, 7)
+HERE, BESIDE = (0, 2, 4, 6), (1, 3, 5, 7)
+ROWS = (0, 2, 1, 3)
+CAPS = (192, 224, 256, 288, 320, 352, 384)
+EARLY = 6
+NT = (((1,), (1,)), ((), ()))
+VMEM = pl.BlockSpec(memory_space=pltpu.VMEM)
+SMEM = pl.BlockSpec(memory_space=pltpu.SMEM)
+HBM = pl.BlockSpec(memory_space=pltpu.HBM)
+
+
+def swap(value, axis, k):
+    n = lax.axis_size(axis)
+    return lax.ppermute(value, axis, [(i, i ^ k) for i in range(n)])
+
+
+def call(body, ins, outs, scratch, limit, *args):
+    return pl.pallas_call(
+        body,
+        in_specs=ins,
+        out_specs=[SMEM if d == jnp.int32 else VMEM for _, d in outs],
+        out_shape=[pltpu.SMEM(s, d) if d == jnp.int32 else pltpu.VMEM(s, d) for s, d in outs],
+        scratch_shapes=scratch,
+        compiler_params=pltpu.CompilerParams(vmem_limit_bytes=limit << 20),
+    )(*(a if spec is SMEM else pltpu.with_memory_space_constraint(a, spec.memory_space) for spec, a in zip(ins, args)))
+
+
+class Columns:
+    def __init__(self, at, w, buf, sems, experts, blocks, width):
+        self.at, self.w, self.buf, self.sems = at, w, buf, sems
+        self.first, self.count, self.blocks, self.width = experts[0], experts[1] - experts[0], blocks, width
+
+    def copy(self, i, j):
+        f_dev, width = self.w.shape[1], self.width
+        col = pl.multiple_of((self.at[0] ^ self.blocks[j]) * width, 128)
+        rows = pl.ds(pl.multiple_of(i * f_dev, f_dev), f_dev)
+        dst = self.buf.at[rows, j * width : (j + 1) * width]
+        return pltpu.make_async_copy(self.w.at[self.first + i, :, pl.ds(col, width)], dst, self.sems.at[i, j])
+
+    def start(self):
+        def one(i, carry):
+            for j in range(len(self.blocks)):
+                self.copy(i, j).start()
+            return carry
+
+        lax.fori_loop(0, self.count, one, 0)
+
+    def wait(self):
+        def one(i, carry):
+            for j in range(len(self.blocks)):
+                self.copy(i, j).wait()
+            return carry
+
+        lax.fori_loop(0, self.count, one, 0)
+
+
+def pre_kernel(tokens, routes, gates, tok, mix, r_buf, g_buf, sems):
+    copies = [
+        pltpu.make_async_copy(src, dst, sems.at[i])
+        for i, (src, dst) in enumerate(((tokens, tok), (routes, r_buf), (gates, g_buf)))
+    ]
+    for c in copies:
+        c.start()
+    for c in copies:
+        c.wait()
+    picked, weights = r_buf[...], g_buf[...].astype(jnp.float32)
+    n = picked.shape[1]
+    ids = lax.broadcasted_iota(jnp.int32, (mix.shape[0], n), 0)
+    total = jnp.zeros(ids.shape, jnp.float32)
+    for k in range(picked.shape[0]):
+        total = total + jnp.where(picked[k : k + 1] == ids, weights[k : k + 1], 0.0)
+    mix[...] = jnp.zeros(mix.shape, mix.dtype)
+    mix[:, :n] = total.astype(mix.dtype)
+
+
+def load_kernel(at, wg, wu, *refs, jobs, width):
+    bufs, sems = refs[: len(jobs)], refs[len(jobs) :]
+    made = [
+        Columns(at, (wg, wu)[which], buf, sem, experts, blocks, width)
+        for (which, experts, blocks), buf, sem in zip(jobs, bufs, sems)
+    ]
+    for c in made:
+        c.start()
+    for c in made:
+        c.wait()
+
+
+def lay(x, mine, other, n_tok, width, second):
+    for r, src in enumerate((mine, mine, other, other)):
+        for j in range(len(HERE)):
+            at = r % 2 * second + j * n_tok
+            x[r * n_tok : (r + 1) * n_tok, j * width : (j + 1) * width] = src[at : at + n_tok, :]
+
+
+def product(acc, pieces, x):
+    base = 0
+    for w in pieces:
+        acc[base : base + w.shape[0], :] = lax.dot_general(w[...], x[...], NT, preferred_element_type=jnp.float32)
+        base += w.shape[0]
+
+
+def early_g_kernel(at, mine, other, g_in, wg, x, g_acc, mix_t, pos_t, pos_c, taken, g_buf, m, sems, *, n_e, f_dev, n_tok, width, caps):
+    made = Columns(at, wg, g_buf, sems, (n_e // 2, n_e), BESIDE, width)
+    made.start()
+    lay(x, mine, other, n_tok, width, mine.shape[0] // 2)
+    product(g_acc, [g_in], x)
+    rows, lanes, block = 4 * n_tok, m.shape[1], mine.shape[0] // 2
+    mix = None
+    for r, src in enumerate((mine, mine, other, other)):
+        lo = r % 2 * block + len(HERE) * n_tok
+        part = src[lo : (r % 2 + 1) * block, :lanes].astype(jnp.float32)
+        part = pltpu.roll(part, r * n_tok, 1) if r else part
+        mix = part if mix is None else mix + part
+    m[: mix.shape[0], :] = mix
+    own = m[pl.ds(at[1] * n_e, n_e), :]
+    mix_t[...] = own
+    member = own > 0.0
+    ones = jnp.where(member, 1.0, 0.0)
+    below = lax.broadcasted_iota(jnp.int32, (rows, rows), 0) < lax.broadcasted_iota(jnp.int32, (rows, rows), 1)
+    below = jnp.where(below, 1.0, 0.0).astype(jnp.bfloat16)
+    rank = jnp.dot(ones.astype(jnp.bfloat16), below, preferred_element_type=jnp.float32)
+    start = jnp.zeros((1, 1), jnp.float32)
+    m[...] = jnp.full(m.shape, -1.0, jnp.float32)
+    for e in range(n_e):
+        m[e : e + 1, :] = jnp.where(member[e : e + 1], rank[e : e + 1] + start, -1.0)
+        start = start + jnp.sum(ones[e : e + 1], axis=1, keepdims=True)
+    pos_t[...] = m[0:n_e, :]
+    columns = m[...].T
+    for e in range(n_e):
+        pos_c[e * rows : (e + 1) * rows, :] = jnp.broadcast_to(columns[:, e : e + 1], (rows, pos_c.shape[1]))
+    total, case = start[0, 0], jnp.int32(0)
+    for cap in caps:
+        case = case + jnp.where(total > cap, 1, 0)
+    taken[0] = case
+    made.wait()
+
+
+def early_u_kernel(at, x, u_in0, u_in1, wu, u_acc, u_buf, sems, *, n_e, f_dev, width):
+    made = Columns(at, wu, u_buf, sems, (0, n_e // 2), BESIDE, width)
+    made.start()
+    product(u_acc, [u_in0, u_in1], x)
+    made.wait()
+
+
+def late_kernel(at, mine, other, g_in0, g_in1, u_in0, wu, g_acc, u_acc, mix_t, pos_t, packed, x, u_in1, sems, *, n_e, f_dev, n_tok, width):
+    made = Columns(at, wu, u_in1, sems, (n_e // 2, n_e), BESIDE, width)
+    made.start()
+    lay(x, mine, other, n_tok, width, mine.shape[0] // 2)
+    slots = lax.broadcasted_iota(jnp.int32, (packed.shape[0], 4 * n_tok), 0).astype(jnp.float32)
+    acc = None
+    for e in range(n_e):
+        side, i = divmod(e, n_e // 2)
+        here = slice(i * f_dev, (i + 1) * f_dev)
+        rows = slice(e * f_dev, (e + 1) * f_dev)
+        g = g_acc[rows] + lax.dot_general((g_in0, g_in1)[side][here], x[...], NT, preferred_element_type=jnp.float32)
+        if e == n_e // 2:
+            made.wait()
+        u = u_acc[rows] + lax.dot_general((u_in0, u_in1)[side][here], x[...], NT, preferred_element_type=jnp.float32)
+        h = (g / (1.0 + jnp.exp(-g)) * u * mix_t[e : e + 1, :]).astype(jnp.bfloat16)
+        pick = jnp.where(slots == pos_t[e : e + 1, :], 1.0, 0.0).astype(jnp.bfloat16)
+        part = lax.dot_general(pick, h, NT, preferred_element_type=jnp.float32)
+        acc = part if acc is None else acc + part
+    packed[...] = acc.astype(jnp.bfloat16)
+
+
+def fetch_kernel(at, wd, d_buf, sems, *, n_e, f_dev):
+    made = []
+    for e in range(n_e):
+        for j, off in enumerate(COLS):
+            row = pl.multiple_of((at[0] ^ off) * f_dev, 128)
+            dst = d_buf.at[e, j * f_dev : (j + 1) * f_dev, :]
+            made.append(pltpu.make_async_copy(wd.at[e, pl.ds(row, f_dev), :], dst, sems.at[e, j]))
+    for c in made:
+        c.start()
+    for c in made:
+        c.wait()
+
+
+def down(acc, blocks, pos, wd, first, unroll):
+    cap, f_dev = blocks[0].shape
+    rows, lanes = acc.shape[0], pos.shape[1]
+    slots = lax.broadcasted_iota(jnp.int32, (rows, lanes), 1).astype(jnp.float32)
+
+    def one(e, carry):
+        here = pos[pl.ds(pl.multiple_of(e * rows, rows), rows), :]
+        place = [jnp.where(slots + float(lo) == here, 1.0, 0.0) for lo in range(0, cap, lanes)]
+        place = jnp.concatenate(place, axis=1)[:, :cap].astype(jnp.bfloat16)
+        h = [jnp.dot(place, b[...], preferred_element_type=jnp.float32).astype(jnp.bfloat16) for b in blocks]
+        units = slice(first * f_dev, (first + len(blocks)) * f_dev)
+        acc[...] += jnp.dot(jnp.concatenate(h, axis=1), wd[e, units, :], preferred_element_type=jnp.float32)
+        return carry
+
+    lax.fori_loop(0, wd.shape[0], one, 0, unroll=unroll)
+
+
+def down_a_kernel(*refs):
+    blocks, (pos, wd, acc) = refs[:EARLY], refs[EARLY:]
+    acc[...] = jnp.zeros(acc.shape, acc.dtype)
+    down(acc, blocks, pos, wd, 0, 1)
+
+
+def down_b_kernel(*refs):
+    late = len(COLS) - EARLY
+    blocks, (pos, wd, acc, out) = refs[:late], refs[late:]
+    out[...] = acc[...]
+    down(out, blocks, pos, wd, EARLY, 2)
+
+
+def planned(tokens, routes, gates, w_gate, w_up, w_down):
+    n_tok, d_dev = tokens.shape
+    n_e, f_dev, _ = w_gate.shape
+    f_all = w_down.shape[1]
+    rows, n = 4 * n_tok, len(COLS)
+    experts = n_e * lax.axis_size("expert")
+    bf16, f32, dma = jnp.bfloat16, jnp.float32, pltpu.SemaphoreType.DMA
+    at = jnp.stack([lax.axis_index("tensor"), lax.axis_index("expert")]).astype(jnp.int32)
+    sizes = dict(n_e=n_e, f_dev=f_dev, width=d_dev)
+    mid, k_half = n_e // 2, len(HERE) * d_dev
+    whole, part = ((n_e * f_dev, k_half), bf16), ((mid * f_dev, k_half), bf16)
+    whole_sems, part_sems = dma((n_e, len(HERE))), dma((mid, len(HERE)))
+    sums = ((n_e * f_dev, rows), f32)
+    half = pltpu.VMEM((rows, len(HERE) * d_dev), bf16)
+    caps = [c for c in CAPS if c < n_e * rows] + [n_e * rows]
+
+    tok, mix = call(
+        pre_kernel, [HBM] * 3, [((n_tok, d_dev), bf16), ((experts, d_dev), bf16)],
+        [pltpu.VMEM(routes.T.shape, jnp.int32), pltpu.VMEM(gates.T.shape, bf16), dma((3,))],
+        4, tokens, routes.T, gates.T,
+    )
+    z2, z4, z6 = (swap(tok, "tensor", k) for k in (2, 4, 6))
+
+    def load(jobs):
+        shapes = [whole if hi - lo == n_e else part for _, (lo, hi), _ in jobs]
+        sems = [whole_sems if hi - lo == n_e else part_sems for _, (lo, hi), _ in jobs]
+        body = functools.partial(load_kernel, jobs=jobs, width=d_dev)
+        return call(body, [SMEM, HBM, HBM], shapes, sems, 4, at, w_gate, w_up)
+
+    g_a, u_a0 = load(((0, (0, n_e), HERE), (1, (0, mid), HERE)))
+    line = jnp.concatenate([tok, z2, z4, z6, mix], axis=0)
+    line_x = swap(line, "expert", 2)
+    line_y = swap(line[:rows], "tensor", 1)
+    u_a1, g_b0 = load(((1, (mid, n_e), HERE), (0, (0, mid), BESIDE)))
+    side_1 = swap(line_x[: rows // 2], "tensor", 1)
+    side_2 = swap(line_y[rows // 2 :], "expert", 2)
+    mine_a = jnp.concatenate([line, line_x], axis=0)
+    other_a = swap(mine_a, "expert", 1)
+    x_a, g_acc, mix_t, pos_t, pos_c, taken, g_b1 = call(
+        functools.partial(early_g_kernel, n_tok=n_tok, caps=caps[:-1], **sizes),
+        [SMEM, VMEM, VMEM, VMEM, HBM],
+        [(half.shape, bf16), sums, ((n_e, rows), f32), ((n_e, rows), f32), ((n_e * rows, 128), f32), ((1,), jnp.int32), part],
+        [pltpu.VMEM((128, rows), f32), part_sems],
+        8, at, mine_a, other_a, g_a, w_gate,
+    )
+    mine_b = jnp.concatenate([line_y, side_1, side_2], axis=0)
+    other_b = swap(mine_b, "expert", 1)
+    u_acc, u_b0 = call(
+        functools.partial(early_u_kernel, **sizes),
+        [SMEM, VMEM, VMEM, VMEM, HBM], [sums, part], [part_sems], 8, at, x_a, u_a0, u_a1, w_up,
+    )
+    (packed,) = call(
+        functools.partial(late_kernel, n_tok=n_tok, **sizes),
+        [SMEM] + [VMEM] * 5 + [HBM] + [VMEM] * 4, [((n_e * rows, f_dev), bf16)],
+        [half, pltpu.VMEM(part[0], bf16), part_sems], 12,
+        at, mine_b, other_b, g_b0, g_b1, u_b0, w_up, g_acc, u_acc, mix_t, pos_t,
+    )
+
+    def finish(cap, packed, pos_c, w_down, at):
+        hidden = packed[:cap]
+        (wd,) = call(
+            functools.partial(fetch_kernel, n_e=n_e, f_dev=f_dev), [SMEM, HBM], [((n_e, f_all, d_dev), bf16)], [dma((n_e, n))], 4, at, w_down
+        )
+        h1 = swap(hidden, "tensor", 1)
+        h2, h4 = (swap(hidden, "tensor", k) for k in (2, 4))
+        h3, h5 = (swap(h, "tensor", 1) for h in (h2, h4))
+        h6, h7 = (swap(h, "tensor", 2) for h in (h4, h5))
+        (acc,) = call(
+            down_a_kernel, [VMEM] * (EARLY + 2), [((rows, d_dev), f32)], [], 16,
+            hidden, h1, h2, h4, h3, h5, pos_c, wd,
+        )
+        return call(
+            down_b_kernel, [VMEM] * (n - EARLY + 3),
+            [((rows, d_dev), f32)], [], 16,
+            h6, h7, pos_c, wd, acc,
+        )[0]
+
+    summed = lax.switch(taken[0], [functools.partial(finish, c) for c in caps], packed, pos_c, w_down, at)
+    total = summed[:n_tok]
+    for j, k in enumerate(ROWS[1:], 1):
+        piece = swap(summed[j * n_tok : (j + 1) * n_tok].astype(bf16), "expert", k)
+        total = total + piece.astype(f32)
+    return total.astype(bf16)
+
+
+def on_device(*args):
+    tokens, _, _, w_gate, _, _ = args
+    n_e, n_t = lax.axis_size("expert"), lax.axis_size("tensor")
+    fits = (n_e, n_t) == (4, 8) and n_e * tokens.shape[0] == CAP
+    tiled = w_gate.shape[0] % 2 == 0 and tokens.shape[0] % 16 == 0 and tokens.shape[1] % 128 == 0 and w_gate.shape[1] % 128 == 0
+    if not (fits and tiled):
+        return general(*args)
+    return planned(*args)
+
+
 def solution(mesh):
     placed = (
         P("expert", "tensor"),

time: 182 us -> 80.2 us (0.44)
  waiting for transfers between devices: 90 us -> 28.7 us
  matrix products: 42 us -> 0 us
  Pallas kernels: 0 us -> 31.3 us
  blocking collectives: 28.9 us -> 0 us
  starting transfers between devices: 0.09 us -> 18.5 us
  between operations: 13.8 us -> 0.18 us
  other arithmetic: 4.59 us -> 0.78 us
    all_gather x2 -> x0, waiting for transfers between devices: 70.4 us -> none  [the longest x1 43.1 us: on_device(): lax.all_gather(hidden, 'tensor', axis=2, tiled=True)]
    dot_general x5 -> x0, matrix products: 42 us -> none  [the longest x1 13 us: on_device(): jnp.einsum('ecd,efd->ecf', slot_rows, w_up, preferred_element_type=jnp.fl...]
    pallas_call x0 -> x9, Pallas kernels: none -> 31.3 us  [call(): pl.pallas_call(body, in_specs=ins, out_specs=[SMEM if d == jnp.int32 else...]
    ppermute x0 -> x19, waiting for transfers between devices: none -> 28.7 us  [swap(): return lax.ppermute(value, axis, [(i, i ^ k) for i in range(n)])]
    all_gather x4 -> x0, blocking collectives: 24.6 us -> none  [the longest x1 8.71 us: on_device(): lax.all_gather(tokens, 'expert', axis=0, tiled=True)]
    reduce_scatter x1 -> x0, waiting for transfers between devices: 19.5 us -> none  [on_device(): lax.psum_scatter(partial_value, 'expert', scatter_dimension=0, tiled=True)]
    ppermute x0 -> x19, starting transfers between devices: none -> 18.5 us  [swap(): return lax.ppermute(value, axis, [(i, i ^ k) for i in range(n)])]
    unnamed x1 -> x0, blocking collectives: 4.26 us -> none
  transfers between devices with their start and end apart: 3 -> 19, of which waited for: 3 -> 9; matrix products, arithmetic and copies ran while one was open for 3% -> 0% of each run, Pallas kernels for 0% -> 29%
where the time goes in v2:
time: 80.2 us; the launch traced here: 80.1 us
  Pallas kernels  31.3 us (39%)
  waiting for transfers between devices  28.7 us (36%)
  starting transfers between devices  18.5 us (23%)
    pallas_call x9, Pallas kernels, call(): pl.pallas_call(body, in_specs=ins, out_specs=[SMEM if d == jnp.int32 else...  31.3 us
    ppermute x19, waiting for transfers between devices, swap(): return lax.ppermute(value, axis, [(i, i ^ k) for i in range(n)])  28.7 us
    ppermute x19, starting transfers between devices, swap(): return lax.ppermute(value, axis, [(i, i ^ k) for i in range(n)])  18.5 us
  transfers between devices with their start and end apart: 19, of which 9 were waited for; matrix products, arithmetic and copies ran while one was open for 0% of the time, Pallas kernels for 29%

profile of v2, /device:TPU:0, one launch (start us, length us, event | category | flops | bytes accessed | tf_op | source)
XLA Modules:
  0.0 80.1 jit_solution(2454688185065103418)
XLA Ops:
  0.0 0.9 %shard_map.72 = (bf16[32,896]{1,0:T(8,128)(2,1)S(1)}, bf16[16,896]{1,0:T(8,128)(2,1)S(1)}) custom-call(bf16[32,896]{1,0:T(8,128)(2,1)} %tokens.1, s32[8,32]{1,0:T(8,128)} %bitcast.5, bf16[8,32]{1,0:T(8,128)(2,1)} %bitcast.6), custom_call_target="tpu_custom_call" | custom-call | tf_op jit(solution)/shard_map/pallas_call | solution.py:93
  0.9 3.1 %collective-permute-start.56 = (bf16[32,896]{1,0:T(8,128)(2,1)S(1)}, bf16[32,896]{1,0:T(8,128)(2,1)S(1)}, u32[]{:S(2)}, u32[]{:S(2)}) collective-permute-start(bf16[32,896]{1,0:T(8,128)(2,1)S(1)} %get-tuple-element.125), channel_id=1, source_target_pairs={{0,2},{1,3},{2,0},{3,1},{4,6},{5,7},{6,4},{7,5},{8,10},{9,11},{10,... | collective-permute-start | bytes 172040 | tf_op jit(solution)/shard_map/ppermute | solution.py:89
  4.0 2.6 %collective-permute-start.57 = (bf16[32,896]{1,0:T(8,128)(2,1)S(1)}, bf16[32,896]{1,0:T(8,128)(2,1)S(1)}, u32[]{:S(2)}, u32[]{:S(2)}) collective-permute-start(bf16[32,896]{1,0:T(8,128)(2,1)S(1)} %get-tuple-element.125), channel_id=1, source_target_pairs={{0,4},{1,5},{2,6},{3,7},{4,0},{5,1},{6,2},{7,3},{8,12},{9,13},{10,... | collective-permute-start | bytes 172040 | tf_op jit(solution)/shard_map/ppermute | solution.py:89
  6.6 3.6 %collective-permute-done.57 = bf16[32,896]{1,0:T(8,128)(2,1)S(1)} collective-permute-done((bf16[32,896]{1,0:T(8,128)(2,1)S(1)}, bf16[32,896]{1,0:T(8,128)(2,1)S(1)}, u32[]{:S(2)}, u32[]{:S(2)}) %collective-permute-start.57) | collective-permute-done | bytes 57376 | tf_op jit(solution)/shard_map/ppermute | solution.py:89
  10.2 2.4 %collective-permute-done.58 = bf16[32,896]{1,0:T(8,128)(2,1)S(1)} collective-permute-done((bf16[32,896]{1,0:T(8,128)(2,1)S(1)}, bf16[32,896]{1,0:T(8,128)(2,1)S(1)}, u32[]{:S(2)}, u32[]{:S(2)}) %collective-permute-start.58) | collective-permute-done | bytes 57376 | tf_op jit(solution)/shard_map/ppermute | solution.py:89
  12.6 1.6 %collective-permute-start.61 = (bf16[128,896]{1,0:T(8,128)(2,1)S(1)}, bf16[128,896]{1,0:T(8,128)(2,1)S(1)}, u32[]{:S(2)}, u32[]{:S(2)}) collective-permute-start(bf16[128,896]{1,0:T(8,128)(2,1)S(1)} %pad_maximum_fusion), channel_id=1, source_target_pairs={{0,1},{1,0},{2,3},{3,2},{4,5},{5,4},{6,7},{7,6},{8,9},{9,8},{10,11... | collective-permute-start | bytes 688136 | tf_op jit(solution)/shard_map/ppermute | solution.py:89
  14.2 1.6 %collective-permute-start.59 = (bf16[144,896]{1,0:T(8,128)(2,1)S(1)}, bf16[144,896]{1,0:T(8,128)(2,1)S(1)}, u32[]{:S(2)}, u32[]{:S(2)}) collective-permute-start(bf16[144,896]{1,0:T(8,128)(2,1)S(1)} %get-tuple-element.167), channel_id=1, source_target_pairs={{0,16},{8,24},{16,0},{24,8},{1,17},{9,25},{17,1},{25,9},{2,18},{10... | collective-permute-start | bytes 774152 | tf_op jit(solution)/shard_map/ppermute | solution.py:89
  15.8 2.9 %collective-permute-done.61 = bf16[128,896]{1,0:T(8,128)(2,1)S(1)} collective-permute-done((bf16[128,896]{1,0:T(8,128)(2,1)S(1)}, bf16[128,896]{1,0:T(8,128)(2,1)S(1)}, u32[]{:S(2)}, u32[]{:S(2)}) %collective-permute-start.61) | collective-permute-done | bytes 229408 | tf_op jit(solution)/shard_map/ppermute | solution.py:89
  18.7 1.6 %collective-permute-start.63 = (bf16[64,896]{1,0:T(8,128)(2,1)S(1)}, bf16[64,896]{1,0:T(8,128)(2,1)S(1)}, u32[]{:S(2)}, u32[]{:S(2)}) collective-permute-start(bf16[64,896]{1,0:T(8,128)(2,1)S(1)} %slice.51), channel_id=1, source_target_pairs={{0,16},{8,24},{16,0},{24,8},{1,17},{9,25},{17,1},{25,9},{2,18},{10... | collective-permute-start | bytes 344072 | tf_op jit(solution)/shard_map/ppermute | solution.py:89
  20.3 1.6 %collective-permute-done.59 = bf16[144,896]{1,0:T(8,128)(2,1)S(1)} collective-permute-done((bf16[144,896]{1,0:T(8,128)(2,1)S(1)}, bf16[144,896]{1,0:T(8,128)(2,1)S(1)}, u32[]{:S(2)}, u32[]{:S(2)}) %collective-permute-start.59) | collective-permute-done | bytes 258080 | tf_op jit(solution)/shard_map/ppermute | solution.py:89
  21.9 0.5 collective-permute-start.62
  22.5 4.2 %collective-permute-done.62 = bf16[64,896]{1,0:T(8,128)(2,1)S(1)} collective-permute-done((bf16[64,896]{1,0:T(8,128)(2,1)S(1)}, bf16[64,896]{1,0:T(8,128)(2,1)S(1)}, u32[]{:S(2)}, u32[]{:S(2)}) %collective-permute-start.62) | collective-permute-done | bytes 114720 | tf_op jit(solution)/shard_map/ppermute | solution.py:89
  26.9 5.0 %shard_map.73 = (bf16[1024,3584]{1,0:T(8,128)(2,1)S(1)}, bf16[512,3584]{1,0:T(8,128)(2,1)S(1)}) custom-call(s32[2]{0:T(128)S(1)} %pad_add_fusion.at, bf16[4,256,7168]{2,1,0:T(8,128)(2,1)} %wg.5, bf16[4,256,7168]{2,1,0:T(8,128)(2,1)} %wu.7), custom_call_target="tpu_custom_call" | custom-call | tf_op jit(solution)/shard_map/pallas_call | solution.py:93
  31.9 3.8 %shard_map.75 = (bf16[512,3584]{1,0:T(8,128)(2,1)S(1)}, bf16[512,3584]{1,0:T(8,128)(2,1)S(1)}) custom-call(s32[2]{0:T(128)S(1)} %pad_add_fusion.at, bf16[4,256,7168]{2,1,0:T(8,128)(2,1)} %wg.5, bf16[4,256,7168]{2,1,0:T(8,128)(2,1)} %wu.7), custom_call_target="tpu_custom_call" | custom-call | tf_op jit(solution)/shard_map/pallas_call | solution.py:93
  35.7 3.0 %shard_map.74 = (bf16[128,3584]{1,0:T(8,128)(2,1)S(1)}, f32[1024,128]{1,0:T(8,128)S(1)}, f32[4,128]{1,0:T(4,128)S(1)}, f32[4,128]{1,0:T(4,128)S(1)}, f32[512,128...) custom-call(s32[2]{0:T(128)S(1)} %pad_add_fusion.at, ...), custom_call_target="tpu_custom_call" | custom-call | tf_op jit(solution)/shard_map/pallas_call | solution.py:93
  38.8 2.7 %shard_map.76 = (f32[1024,128]{1,0:T(8,128)S(1)}, bf16[512,3584]{1,0:T(8,128)(2,1)S(1)}) custom-call(s32[2]{0:T(128)S(1)} %pad_add_fusion.at, bf16[128,3584]{1,0:T(8,128)(2,1)S(1)} %get-tuple-element.131.x, bf16[512,3584]{1,0:T(8,128)(2,1)S(1)} %get-tuple-element.132.u_in0, bf16[512,3584]{1,0:T(8,128)(2,1)S(1)} %get-tuple-element.133.u_in1, ...), custom_call_target="tpu_custom_call" | custom-call | tf_op jit(solution)/shard_map/pallas_call | solution.py:93
  41.5 5.6 %shard_map.77 = bf16[512,256]{1,0:T(8,128)(2,1)S(1)} custom-call(s32[2]{0:T(128)S(1)} %pad_add_fusion.at, bf16[256,896]{1,0:T(8,128)(2,1)S(1)} %constant_dynamic-update-slice_fusion.11.mine, bf16[256,896]{1,0:T(8,128)(2,1)S(1)} %collective-permute-done.64.other, bf16[512,3584]{1,0:T(8,128)(2,1)S(1)} %get-tuple-element.129.g_in0, ...), custom_call_target="tpu_custom_call" | custom-call | tf_op jit(solution)/shard_map/pallas_call | solution.py:93
  47.1 25.7 %conditional.1 = (f32[128,896]{1,0:T(8,128)S(1)}) conditional(s32[]{:T(128)} %bitcast.4, (bf16[512,256]{1,0:T(8,128)(2,1)S(1)}, s32[2]{0:T(128)S(1)}, bf16[4,2048,896]{2,1,0:T(8,128)(2,1)}, f32[512,128]{1,0:T(8,128)S(1)}) %tuple.29, (bf16[512,256]{1,0:T(8,128)(2,1)S(1)}, s32[2]{0:T(128)S(1)}, ...), branch_computations={%region_0.0_spmd, %region_1.0_spmd, %region_2.0_spmd, %region_3.0_... | conditional | bytes 7340320 | solution.py:361
  47.2 1.3 %collective-permute-start.7 = (bf16[224,256]{1,0:T(8,128)(2,1)S(1)}, bf16[224,256]{1,0:T(8,128)(2,1)S(1)}, u32[]{:S(2)}, u32[]{:S(2)}) collective-permute-start(bf16[224,256]{1,0:T(8,128)(2,1)S(1)} %slice.32.refs_0_), channel_id=1, source_target_pairs={{0,4},{1,5},{2,6},{3,7},{4,0},{5,1},{6,2},{7,3},{8,12},{9,13},{10,... | collective-permute-start | bytes 344072 | tf_op jit(solution)/shard_map/cond/branch_1_fun/ppermute | solution.py:89
  48.5 0.6 collective-permute-start.12
  49.1 7.0 %collective-permute-done.7.refs_3_ = bf16[224,256]{1,0:T(8,128)(2,1)S(1)} collective-permute-done((bf16[224,256]{1,0:T(8,128)(2,1)S(1)}, bf16[224,256]{1,0:T(8,128)(2,1)S(1)}, u32[]{:S(2)}, u32[]{:S(2)}) %collective-permute-start.7) | collective-permute-done | bytes 114720 | tf_op jit(solution)/shard_map/cond/branch_1_fun/ppermute | solution.py:89
  56.1 0.3 collective-permute-start.9
  56.4 1.7 %collective-permute-start.11 = (bf16[224,256]{1,0:T(8,128)(2,1)S(1)}, bf16[224,256]{1,0:T(8,128)(2,1)S(1)}, u32[]{:S(2)}, u32[]{:S(2)}) collective-permute-start(bf16[224,256]{1,0:T(8,128)(2,1)S(1)} %slice.32.refs_0_), channel_id=1, source_target_pairs={{0,1},{1,0},{2,3},{3,2},{4,5},{5,4},{6,7},{7,6},{8,9},{9,8},{10,11... | collective-permute-start | bytes 344072 | tf_op jit(solution)/shard_map/cond/branch_1_fun/ppermute | solution.py:89
  58.1 0.3 collective-permute-start.13
  58.4 3.6 %collective-permute-done.9.refs_5_ = bf16[224,256]{1,0:T(8,128)(2,1)S(1)} collective-permute-done((bf16[224,256]{1,0:T(8,128)(2,1)S(1)}, bf16[224,256]{1,0:T(8,128)(2,1)S(1)}, u32[]{:S(2)}, u32[]{:S(2)}) %collective-permute-start.9) | collective-permute-done | bytes 114720 | tf_op jit(solution)/shard_map/cond/branch_1_fun/ppermute | solution.py:89
  62.1 6.0 %branch_1_fun.3.refs_7_.refs_3_ = bf16[4,2048,896]{2,1,0:T(8,128)(2,1)S(1)} custom-call(s32[2]{0:T(128)S(1)} %get-tuple-element.84.at, bf16[4,2048,896]{2,1,0:T(8,128)(2,1)} %get-tuple-element.149.wd), custom_call_target="tpu_custom_call" | custom-call | tf_op jit(solution)/shard_map/cond/branch_1_fun/pallas_call | solution.py:93
  68.1 2.8 %branch_1_fun.4.refs_4_ = f32[128,896]{1,0:T(8,128)S(1)} custom-call(bf16[224,256]{1,0:T(8,128)(2,1)S(1)} %slice.32.refs_0_, bf16[224,256]{1,0:T(8,128)(2,1)S(1)} %collective-permute-done.11.refs_1_, bf16[224,256]{1,0:T(8,128)(2,1)S(1)} %collective-permute-done.12.refs_2_, bf16[224,256]{1,0:T(8,128)(2,1)S(1)} %collective-permute-done.7.refs_3_, ...), custom_call_target="tpu_custom_call" | custom-call | tf_op jit(solution)/shard_map/cond/branch_1_fun/pallas_call | solution.py:93
  70.9 1.5 %branch_1_fun.5 = f32[128,896]{1,0:T(8,128)S(1)} custom-call(bf16[224,256]{1,0:T(8,128)(2,1)S(1)} %collective-permute-done.8.refs_0_, bf16[224,256]{1,0:T(8,128)(2,1)S(1)} %collective-permute-done.10.refs_1_, f32[512,128]{1,0:T(8,128)S(1)} %get-tuple-element.82.refs_6_.refs_2_, bf16[4,2048,896]{2,1,0:T(8,128)(2,1)S(1)} %branch_1_fun.3.refs_7_.refs_3_, ...), custom_call_target="tpu_custom_call" | custom-call | tf_op jit(solution)/shard_map/cond/branch_1_fun/pallas_call | solution.py:93
  72.9 2.9 %collective-permute-start.65 = (bf16[32,896]{1,0:T(8,128)(2,1)S(1)}, bf16[32,896]{1,0:T(8,128)(2,1)S(1)}, u32[]{:S(2)}, u32[]{:S(2)}) collective-permute-start(bf16[32,896]{1,0:T(8,128)(2,1)S(1)} %get-tuple-element.156), channel_id=1, source_target_pairs={{0,16},{8,24},{16,0},{24,8},{1,17},{9,25},{17,1},{25,9},{2,18},{10... | collective-permute-start | bytes 172040 | tf_op jit(solution)/shard_map/ppermute | solution.py:89
  76.0 2.0 %collective-permute-done.65 = bf16[32,896]{1,0:T(8,128)(2,1)S(1)} collective-permute-done((bf16[32,896]{1,0:T(8,128)(2,1)S(1)}, bf16[32,896]{1,0:T(8,128)(2,1)S(1)}, u32[]{:S(2)}, u32[]{:S(2)}) %collective-permute-start.65) | collective-permute-done | bytes 57376 | tf_op jit(solution)/shard_map/ppermute | solution.py:89
  78.0 1.4 %collective-permute-done.67 = bf16[32,896]{1,0:T(8,128)(2,1)S(1)} collective-permute-done((bf16[32,896]{1,0:T(8,128)(2,1)S(1)}, bf16[32,896]{1,0:T(8,128)(2,1)S(1)}, u32[]{:S(2)}, u32[]{:S(2)}) %collective-permute-start.67) | collective-permute-done | bytes 57376 | tf_op jit(solution)/shard_map/ppermute | solution.py:89
  79.4 0.7 fusion.2
  (33 shorter events, 0.7 us)
Async XLA Ops:
  0.9 5.7 %collective-permute-start.56 = (bf16[32,896]{1,0:T(8,128)(2,1)S(1)}, bf16[32,896]{1,0:T(8,128)(2,1)S(1)}, u32[]{:S(2)}, u32[]{:S(2)}) collective-permute-start(bf16[32,896]{1,0:T(8,128)(2,1)S(1)} %get-tuple-element.125), channel_id=1, source_target_pairs={{0,2},{1,3},{2,0},{3,1},{4,6},{5,7},{6,4},{7,5},{8,10},{9,11},{10,... | collective-permute-start | bytes 172040 | tf_op jit(solution)/shard_map/ppermute | solution.py:89
  4.0 6.2 %collective-permute-start.57 = (bf16[32,896]{1,0:T(8,128)(2,1)S(1)}, bf16[32,896]{1,0:T(8,128)(2,1)S(1)}, u32[]{:S(2)}, u32[]{:S(2)}) collective-permute-start(bf16[32,896]{1,0:T(8,128)(2,1)S(1)} %get-tuple-element.125), channel_id=1, source_target_pairs={{0,4},{1,5},{2,6},{3,7},{4,0},{5,1},{6,2},{7,3},{8,12},{9,13},{10,... | collective-permute-start | bytes 172040 | tf_op jit(solution)/shard_map/ppermute | solution.py:89
  6.6 6.0 %collective-permute-start.58 = (bf16[32,896]{1,0:T(8,128)(2,1)S(1)}, bf16[32,896]{1,0:T(8,128)(2,1)S(1)}, u32[]{:S(2)}, u32[]{:S(2)}) collective-permute-start(bf16[32,896]{1,0:T(8,128)(2,1)S(1)} %get-tuple-element.125), channel_id=1, source_target_pairs={{0,6},{1,7},{2,4},{3,5},{4,2},{5,3},{6,0},{7,1},{8,14},{9,15},{10,... | collective-permute-start | bytes 172040 | tf_op jit(solution)/shard_map/ppermute | solution.py:89
  12.6 6.1 %collective-permute-start.61 = (bf16[128,896]{1,0:T(8,128)(2,1)S(1)}, bf16[128,896]{1,0:T(8,128)(2,1)S(1)}, u32[]{:S(2)}, u32[]{:S(2)}) collective-permute-start(bf16[128,896]{1,0:T(8,128)(2,1)S(1)} %pad_maximum_fusion), channel_id=1, source_target_pairs={{0,1},{1,0},{2,3},{3,2},{4,5},{5,4},{6,7},{7,6},{8,9},{9,8},{10,11... | collective-permute-start | bytes 688136 | tf_op jit(solution)/shard_map/ppermute | solution.py:89
  14.2 7.6 %collective-permute-start.59 = (bf16[144,896]{1,0:T(8,128)(2,1)S(1)}, bf16[144,896]{1,0:T(8,128)(2,1)S(1)}, u32[]{:S(2)}, u32[]{:S(2)}) collective-permute-start(bf16[144,896]{1,0:T(8,128)(2,1)S(1)} %get-tuple-element.167), channel_id=1, source_target_pairs={{0,16},{8,24},{16,0},{24,8},{1,17},{9,25},{17,1},{25,9},{2,18},{10... | collective-permute-start | bytes 774152 | tf_op jit(solution)/shard_map/ppermute | solution.py:89
  18.7 8.1 %collective-permute-start.63 = (bf16[64,896]{1,0:T(8,128)(2,1)S(1)}, bf16[64,896]{1,0:T(8,128)(2,1)S(1)}, u32[]{:S(2)}, u32[]{:S(2)}) collective-permute-start(bf16[64,896]{1,0:T(8,128)(2,1)S(1)} %slice.51), channel_id=1, source_target_pairs={{0,16},{8,24},{16,0},{24,8},{1,17},{9,25},{17,1},{25,9},{2,18},{10... | collective-permute-start | bytes 344072 | tf_op jit(solution)/shard_map/ppermute | solution.py:89
  21.9 4.9 %collective-permute-start.62 = (bf16[64,896]{1,0:T(8,128)(2,1)S(1)}, bf16[64,896]{1,0:T(8,128)(2,1)S(1)}, u32[]{:S(2)}, u32[]{:S(2)}) collective-permute-start(bf16[64,896]{1,0:T(8,128)(2,1)S(1)} %slice.50), channel_id=1, source_target_pairs={{0,1},{1,0},{2,3},{3,2},{4,5},{5,4},{6,7},{7,6},{8,9},{9,8},{10,11... | collective-permute-start | bytes 344072 | tf_op jit(solution)/shard_map/ppermute | solution.py:89
  22.5 13.3 %collective-permute-start.60 = (bf16[288,896]{1,0:T(8,128)(2,1)S(1)}, bf16[288,896]{1,0:T(8,128)(2,1)S(1)}, u32[]{:S(2)}, u32[]{:S(2)}) collective-permute-start(bf16[288,896]{1,0:T(8,128)(2,1)S(1)} %constant_dynamic-update-slice_fusion.5.mine), channel_id=1, source_target_pairs={{0,8},{8,0},{16,24},{24,16},{1,9},{9,1},{17,25},{25,17},{2,10},{10... | collective-permute-start | bytes 1548296 | tf_op jit(solution)/shard_map/ppermute | solution.py:89
  26.8 14.7 %collective-permute-start.64 = (bf16[256,896]{1,0:T(8,128)(2,1)S(1)}, bf16[256,896]{1,0:T(8,128)(2,1)S(1)}, u32[]{:S(2)}, u32[]{:S(2)}) collective-permute-start(bf16[256,896]{1,0:T(8,128)(2,1)S(1)} %constant_dynamic-update-slice_fusion.11.mine), channel_id=1, source_target_pairs={{0,8},{8,0},{16,24},{24,16},{1,9},{9,1},{17,25},{25,17},{2,10},{10... | collective-permute-start | bytes 1376264 | tf_op jit(solution)/shard_map/ppermute | solution.py:89
  47.2 8.9 %collective-permute-start.7 = (bf16[224,256]{1,0:T(8,128)(2,1)S(1)}, bf16[224,256]{1,0:T(8,128)(2,1)S(1)}, u32[]{:S(2)}, u32[]{:S(2)}) collective-permute-start(bf16[224,256]{1,0:T(8,128)(2,1)S(1)} %slice.32.refs_0_), channel_id=1, source_target_pairs={{0,4},{1,5},{2,6},{3,7},{4,0},{5,1},{6,2},{7,3},{8,12},{9,13},{10,... | collective-permute-start | bytes 344072 | tf_op jit(solution)/shard_map/cond/branch_1_fun/ppermute | solution.py:89
  48.5 9.6 %collective-permute-start.12 = (bf16[224,256]{1,0:T(8,128)(2,1)S(1)}, bf16[224,256]{1,0:T(8,128)(2,1)S(1)}, u32[]{:S(2)}, u32[]{:S(2)}) collective-permute-start(bf16[224,256]{1,0:T(8,128)(2,1)S(1)} %slice.32.refs_0_), channel_id=1, source_target_pairs={{0,2},{1,3},{2,0},{3,1},{4,6},{5,7},{6,4},{7,5},{8,10},{9,11},{10,... | collective-permute-start | bytes 344072 | tf_op jit(solution)/shard_map/cond/branch_1_fun/ppermute | solution.py:89
  56.1 6.0 %collective-permute-start.9 = (bf16[224,256]{1,0:T(8,128)(2,1)S(1)}, bf16[224,256]{1,0:T(8,128)(2,1)S(1)}, u32[]{:S(2)}, u32[]{:S(2)}) collective-permute-start(bf16[224,256]{1,0:T(8,128)(2,1)S(1)} %collective-permute-done.7.refs_3_), channel_id=1, source_target_pairs={{0,1},{1,0},{2,3},{3,2},{4,5},{5,4},{6,7},{7,6},{8,9},{9,8},{10,11... | collective-permute-start | bytes 344072 | tf_op jit(solution)/shard_map/cond/branch_1_fun/ppermute | solution.py:89
  56.4 11.7 %collective-permute-start.11 = (bf16[224,256]{1,0:T(8,128)(2,1)S(1)}, bf16[224,256]{1,0:T(8,128)(2,1)S(1)}, u32[]{:S(2)}, u32[]{:S(2)}) collective-permute-start(bf16[224,256]{1,0:T(8,128)(2,1)S(1)} %slice.32.refs_0_), channel_id=1, source_target_pairs={{0,1},{1,0},{2,3},{3,2},{4,5},{5,4},{6,7},{7,6},{8,9},{9,8},{10,11... | collective-permute-start | bytes 344072 | tf_op jit(solution)/shard_map/cond/branch_1_fun/ppermute | solution.py:89
  58.1 10.0 %collective-permute-start.13 = (bf16[224,256]{1,0:T(8,128)(2,1)S(1)}, bf16[224,256]{1,0:T(8,128)(2,1)S(1)}, u32[]{:S(2)}, u32[]{:S(2)}) collective-permute-start(bf16[224,256]{1,0:T(8,128)(2,1)S(1)} %collective-permute-done.12.refs_2_), channel_id=1, source_target_pairs={{0,1},{1,0},{2,3},{3,2},{4,5},{5,4},{6,7},{7,6},{8,9},{9,8},{10,11... | collective-permute-start | bytes 344072 | tf_op jit(solution)/shard_map/cond/branch_1_fun/ppermute | solution.py:89
  58.4 12.5 %collective-permute-start.8 = (bf16[224,256]{1,0:T(8,128)(2,1)S(1)}, bf16[224,256]{1,0:T(8,128)(2,1)S(1)}, u32[]{:S(2)}, u32[]{:S(2)}) collective-permute-start(bf16[224,256]{1,0:T(8,128)(2,1)S(1)} %collective-permute-done.7.refs_3_), channel_id=1, source_target_pairs={{0,2},{1,3},{2,0},{3,1},{4,6},{5,7},{6,4},{7,5},{8,10},{9,11},{10,... | collective-permute-start | bytes 344072 | tf_op jit(solution)/shard_map/cond/branch_1_fun/ppermute | solution.py:89
  62.1 8.9 %collective-permute-start.10 = (bf16[224,256]{1,0:T(8,128)(2,1)S(1)}, bf16[224,256]{1,0:T(8,128)(2,1)S(1)}, u32[]{:S(2)}, u32[]{:S(2)}) collective-permute-start(bf16[224,256]{1,0:T(8,128)(2,1)S(1)} %collective-permute-done.9.refs_5_), channel_id=1, source_target_pairs={{0,2},{1,3},{2,0},{3,1},{4,6},{5,7},{6,4},{7,5},{8,10},{9,11},{10,... | collective-permute-start | bytes 344072 | tf_op jit(solution)/shard_map/cond/branch_1_fun/ppermute | solution.py:89
  72.9 5.1 %collective-permute-start.65 = (bf16[32,896]{1,0:T(8,128)(2,1)S(1)}, bf16[32,896]{1,0:T(8,128)(2,1)S(1)}, u32[]{:S(2)}, u32[]{:S(2)}) collective-permute-start(bf16[32,896]{1,0:T(8,128)(2,1)S(1)} %get-tuple-element.156), channel_id=1, source_target_pairs={{0,16},{8,24},{16,0},{24,8},{1,17},{9,25},{17,1},{25,9},{2,18},{10... | collective-permute-start | bytes 172040 | tf_op jit(solution)/shard_map/ppermute | solution.py:89
  75.8 2.2 %collective-permute-start.66 = (bf16[32,896]{1,0:T(8,128)(2,1)S(1)}, bf16[32,896]{1,0:T(8,128)(2,1)S(1)}, u32[]{:S(2)}, u32[]{:S(2)}) collective-permute-start(bf16[32,896]{1,0:T(8,128)(2,1)S(1)} %get-tuple-element.158), channel_id=1, source_target_pairs={{0,8},{8,0},{16,24},{24,16},{1,9},{9,1},{17,25},{25,17},{2,10},{10... | collective-permute-start | bytes 172040 | tf_op jit(solution)/shard_map/ppermute | solution.py:89
  75.8 3.6 %collective-permute-start.67 = (bf16[32,896]{1,0:T(8,128)(2,1)S(1)}, bf16[32,896]{1,0:T(8,128)(2,1)S(1)}, u32[]{:S(2)}, u32[]{:S(2)}) collective-permute-start(bf16[32,896]{1,0:T(8,128)(2,1)S(1)} %get-tuple-element.157), channel_id=1, source_target_pairs={{0,24},{8,16},{16,8},{24,0},{1,25},{9,17},{17,9},{25,1},{2,26},{10... | collective-permute-start | bytes 172040 | tf_op jit(solution)/shard_map/ppermute | solution.py:89

commit v3 on v2

--- a/solution.py
+++ b/solution.py
@@ -76,7 +76,7 @@
 COLS = (0, 1, 2, 4, 3, 5, 6, 7)
 HERE, BESIDE = (0, 2, 4, 6), (1, 3, 5, 7)
 ROWS = (0, 2, 1, 3)
-CAPS = (192, 224, 256, 288, 320, 352, 384)
+CAPS = (192, 224, 256, 288, 304, 320, 336, 352, 384)
 EARLY = 6
 NT = (((1,), (1,)), ((), ()))
 VMEM = pl.BlockSpec(memory_space=pltpu.VMEM)
@@ -238,21 +238,30 @@
     packed[...] = acc.astype(jnp.bfloat16)
 
 
-def fetch_kernel(at, wd, d_buf, sems, *, n_e, f_dev):
-    made = []
-    for e in range(n_e):
-        for j, off in enumerate(COLS):
-            row = pl.multiple_of((at[0] ^ off) * f_dev, 128)
-            dst = d_buf.at[e, j * f_dev : (j + 1) * f_dev, :]
-            made.append(pltpu.make_async_copy(wd.at[e, pl.ds(row, f_dev), :], dst, sems.at[e, j]))
-    for c in made:
-        c.start()
-    for c in made:
-        c.wait()
-
-
-def down(acc, blocks, pos, wd, first, unroll):
-    cap, f_dev = blocks[0].shape
+class Rows:
+    def __init__(self, at, w, buf, sems, first, f_dev):
+        self.at, self.w, self.buf, self.sems, self.f_dev = at, w, buf, sems, f_dev
+        self.blocks = COLS[first : first + buf.shape[1] // f_dev]
+
+    def each(self, act):
+        def one(e, carry):
+            for j, off in enumerate(self.blocks):
+                row = pl.multiple_of((self.at[0] ^ off) * self.f_dev, 128)
+                dst = self.buf.at[e, j * self.f_dev : (j + 1) * self.f_dev, :]
+                act(pltpu.make_async_copy(self.w.at[e, pl.ds(row, self.f_dev), :], dst, self.sems.at[e, j]))
+            return carry
+
+        lax.fori_loop(0, self.buf.shape[0], one, 0)
+
+
+def fetch_kernel(at, wd, buf, sems, *, first, f_dev):
+    rows = Rows(at, wd, buf, sems, first, f_dev)
+    rows.each(lambda c: c.start())
+    rows.each(lambda c: c.wait())
+
+
+def down(acc, blocks, pos, w, unroll):
+    cap, _ = blocks[0].shape
     rows, lanes = acc.shape[0], pos.shape[1]
     slots = lax.broadcasted_iota(jnp.int32, (rows, lanes), 1).astype(jnp.float32)
 
@@ -261,30 +270,31 @@
         place = [jnp.where(slots + float(lo) == here, 1.0, 0.0) for lo in range(0, cap, lanes)]
         place = jnp.concatenate(place, axis=1)[:, :cap].astype(jnp.bfloat16)
         h = [jnp.dot(place, b[...], preferred_element_type=jnp.float32).astype(jnp.bfloat16) for b in blocks]
-        units = slice(first * f_dev, (first + len(blocks)) * f_dev)
-        acc[...] += jnp.dot(jnp.concatenate(h, axis=1), wd[e, units, :], preferred_element_type=jnp.float32)
+        acc[...] += jnp.dot(jnp.concatenate(h, axis=1), w[e], preferred_element_type=jnp.float32)
         return carry
 
-    lax.fori_loop(0, wd.shape[0], one, 0, unroll=unroll)
-
-
-def down_a_kernel(*refs):
-    blocks, (pos, wd, acc) = refs[:EARLY], refs[EARLY:]
+    lax.fori_loop(0, w.shape[0], one, 0, unroll=unroll)
+
+
+def down_a_kernel(at, *refs):
+    blocks, (pos, w, wd, acc, buf, sems) = refs[:EARLY], refs[EARLY:]
+    rows = Rows(at, wd, buf, sems, EARLY, blocks[0].shape[1])
+    rows.each(lambda c: c.start())
     acc[...] = jnp.zeros(acc.shape, acc.dtype)
-    down(acc, blocks, pos, wd, 0, 1)
+    down(acc, blocks, pos, w, 1)
+    rows.each(lambda c: c.wait())
 
 
 def down_b_kernel(*refs):
     late = len(COLS) - EARLY
-    blocks, (pos, wd, acc, out) = refs[:late], refs[late:]
+    blocks, (pos, w2, acc, out) = refs[:late], refs[late:]
     out[...] = acc[...]
-    down(out, blocks, pos, wd, EARLY, 2)
+    down(out, blocks, pos, w2, 2)
 
 
 def planned(tokens, routes, gates, w_gate, w_up, w_down):
     n_tok, d_dev = tokens.shape
     n_e, f_dev, _ = w_gate.shape
-    f_all = w_down.shape[1]
     rows, n = 4 * n_tok, len(COLS)
     experts = n_e * lax.axis_size("expert")
     bf16, f32, dma = jnp.bfloat16, jnp.float32, pltpu.SemaphoreType.DMA
@@ -302,7 +312,7 @@
         [pltpu.VMEM(routes.T.shape, jnp.int32), pltpu.VMEM(gates.T.shape, bf16), dma((3,))],
         4, tokens, routes.T, gates.T,
     )
-    z2, z4, z6 = (swap(tok, "tensor", k) for k in (2, 4, 6))
+    z2, z4, z6 = (swap(tokens, "tensor", k) for k in (2, 4, 6))
 
     def load(jobs):
         shapes = [whole if hi - lo == n_e else part for _, (lo, hi), _ in jobs]
@@ -341,22 +351,20 @@
 
     def finish(cap, packed, pos_c, w_down, at):
         hidden = packed[:cap]
-        (wd,) = call(
-            functools.partial(fetch_kernel, n_e=n_e, f_dev=f_dev), [SMEM, HBM], [((n_e, f_all, d_dev), bf16)], [dma((n_e, n))], 4, at, w_down
+        (w,) = call(
+            functools.partial(fetch_kernel, first=0, f_dev=f_dev),
+            [SMEM, HBM], [((n_e, EARLY * f_dev, d_dev), bf16)], [dma((n_e, EARLY))], 4, at, w_down,
         )
         h1 = swap(hidden, "tensor", 1)
         h2, h4 = (swap(hidden, "tensor", k) for k in (2, 4))
         h3, h5 = (swap(h, "tensor", 1) for h in (h2, h4))
         h6, h7 = (swap(h, "tensor", 2) for h in (h4, h5))
-        (acc,) = call(
-            down_a_kernel, [VMEM] * (EARLY + 2), [((rows, d_dev), f32)], [], 16,
-            hidden, h1, h2, h4, h3, h5, pos_c, wd,
+        acc, w2 = call(
+            down_a_kernel, [SMEM] + [VMEM] * (EARLY + 2) + [HBM],
+            [((rows, d_dev), f32), ((n_e, (n - EARLY) * f_dev, d_dev), bf16)], [dma((n_e, n - EARLY))], 16,
+            at, hidden, h1, h2, h4, h3, h5, pos_c, w, w_down,
         )
-        return call(
-            down_b_kernel, [VMEM] * (n - EARLY + 3),
-            [((rows, d_dev), f32)], [], 16,
-            h6, h7, pos_c, wd, acc,
-        )[0]
+        return call(down_b_kernel, [VMEM] * (n - EARLY + 3), [((rows, d_dev), f32)], [], 16, h6, h7, pos_c, w2, acc)[0]
 
     summed = lax.switch(taken[0], [functools.partial(finish, c) for c in caps], packed, pos_c, w_down, at)
     total = summed[:n_tok]

time: 80.2 us -> 79.1 us (0.986)
  transfers between devices with their start and end apart: 19 -> 19, of which waited for: 9 -> 9; matrix products, arithmetic and copies ran while one was open for 0% -> 0% of each run, Pallas kernels for 29% -> 30%
where the time goes in v3:
time: 79.1 us; the launch traced here: 78.9 us
  Pallas kernels  30.9 us (39%)
  waiting for transfers between devices  27.9 us (35%)
  starting transfers between devices  18.5 us (23%)
    pallas_call x9, Pallas kernels, call(): pl.pallas_call(body, in_specs=ins, out_specs=[SMEM if d == jnp.int32 else...  30.9 us
    ppermute x19, waiting for transfers between devices, swap(): return lax.ppermute(value, axis, [(i, i ^ k) for i in range(n)])  27.9 us
    ppermute x19, starting transfers between devices, swap(): return lax.ppermute(value, axis, [(i, i ^ k) for i in range(n)])  18.5 us
  transfers between devices with their start and end apart: 19, of which 9 were waited for; matrix products, arithmetic and copies ran while one was open for 0% of the time, Pallas kernels for 30%

profile of v3, /device:TPU:0, one launch (start us, length us, event | category | flops | bytes accessed | tf_op | source)
XLA Modules:
  0.0 78.9 jit_solution(17325914232590057079)
XLA Ops:
  0.0 3.1 %collective-permute-start.70 = (bf16[32,896]{1,0:T(8,128)(2,1)}, bf16[32,896]{1,0:T(8,128)(2,1)S(1)}, u32[]{:S(2)}, u32[]{:S(2)}) collective-permute-start(bf16[32,896]{1,0:T(8,128)(2,1)} %tokens.1), channel_id=1, source_target_pairs={{0,2},{1,3},{2,0},{3,1},{4,6},{5,7},{6,4},{7,5},{8,10},{9,11},{10,... | collective-permute-start | bytes 172040 | tf_op jit(solution)/shard_map/ppermute | solution.py:89
  3.1 2.6 %collective-permute-start.71 = (bf16[32,896]{1,0:T(8,128)(2,1)}, bf16[32,896]{1,0:T(8,128)(2,1)S(1)}, u32[]{:S(2)}, u32[]{:S(2)}) collective-permute-start(bf16[32,896]{1,0:T(8,128)(2,1)} %tokens.1), channel_id=1, source_target_pairs={{0,4},{1,5},{2,6},{3,7},{4,0},{5,1},{6,2},{7,3},{8,12},{9,13},{10,... | collective-permute-start | bytes 172040 | tf_op jit(solution)/shard_map/ppermute | solution.py:89
  5.6 0.9 %shard_map.74 = (bf16[32,896]{1,0:T(8,128)(2,1)S(1)}, bf16[16,896]{1,0:T(8,128)(2,1)S(1)}) custom-call(bf16[32,896]{1,0:T(8,128)(2,1)} %tokens.1, s32[8,32]{1,0:T(8,128)} %bitcast.5, bf16[8,32]{1,0:T(8,128)(2,1)} %bitcast.6), custom_call_target="tpu_custom_call" | custom-call | tf_op jit(solution)/shard_map/pallas_call | solution.py:93
  6.6 2.8 %collective-permute-done.71 = bf16[32,896]{1,0:T(8,128)(2,1)S(1)} collective-permute-done((bf16[32,896]{1,0:T(8,128)(2,1)}, bf16[32,896]{1,0:T(8,128)(2,1)S(1)}, u32[]{:S(2)}, u32[]{:S(2)}) %collective-permute-start.71) | collective-permute-done | bytes 57376 | tf_op jit(solution)/shard_map/ppermute | solution.py:89
  9.5 2.4 %collective-permute-done.72 = bf16[32,896]{1,0:T(8,128)(2,1)S(1)} collective-permute-done((bf16[32,896]{1,0:T(8,128)(2,1)}, bf16[32,896]{1,0:T(8,128)(2,1)S(1)}, u32[]{:S(2)}, u32[]{:S(2)}) %collective-permute-start.72) | collective-permute-done | bytes 57376 | tf_op jit(solution)/shard_map/ppermute | solution.py:89
  11.9 1.6 %collective-permute-start.75 = (bf16[128,896]{1,0:T(8,128)(2,1)S(1)}, bf16[128,896]{1,0:T(8,128)(2,1)S(1)}, u32[]{:S(2)}, u32[]{:S(2)}) collective-permute-start(bf16[128,896]{1,0:T(8,128)(2,1)S(1)} %pad_maximum_fusion), channel_id=1, source_target_pairs={{0,1},{1,0},{2,3},{3,2},{4,5},{5,4},{6,7},{7,6},{8,9},{9,8},{10,11... | collective-permute-start | bytes 688136 | tf_op jit(solution)/shard_map/ppermute | solution.py:89
  13.5 1.6 %collective-permute-start.73 = (bf16[144,896]{1,0:T(8,128)(2,1)S(1)}, bf16[144,896]{1,0:T(8,128)(2,1)S(1)}, u32[]{:S(2)}, u32[]{:S(2)}) collective-permute-start(bf16[144,896]{1,0:T(8,128)(2,1)S(1)} %get-tuple-element.217), channel_id=1, source_target_pairs={{0,16},{8,24},{16,0},{24,8},{1,17},{9,25},{17,1},{25,9},{2,18},{10... | collective-permute-start | bytes 774152 | tf_op jit(solution)/shard_map/ppermute | solution.py:89
  15.1 2.9 %collective-permute-done.75 = bf16[128,896]{1,0:T(8,128)(2,1)S(1)} collective-permute-done((bf16[128,896]{1,0:T(8,128)(2,1)S(1)}, bf16[128,896]{1,0:T(8,128)(2,1)S(1)}, u32[]{:S(2)}, u32[]{:S(2)}) %collective-permute-start.75) | collective-permute-done | bytes 229408 | tf_op jit(solution)/shard_map/ppermute | solution.py:89
  18.0 1.6 %collective-permute-start.77 = (bf16[64,896]{1,0:T(8,128)(2,1)S(1)}, bf16[64,896]{1,0:T(8,128)(2,1)S(1)}, u32[]{:S(2)}, u32[]{:S(2)}) collective-permute-start(bf16[64,896]{1,0:T(8,128)(2,1)S(1)} %slice.57), channel_id=1, source_target_pairs={{0,16},{8,24},{16,0},{24,8},{1,17},{9,25},{17,1},{25,9},{2,18},{10... | collective-permute-start | bytes 344072 | tf_op jit(solution)/shard_map/ppermute | solution.py:89
  19.5 1.6 %collective-permute-done.73 = bf16[144,896]{1,0:T(8,128)(2,1)S(1)} collective-permute-done((bf16[144,896]{1,0:T(8,128)(2,1)S(1)}, bf16[144,896]{1,0:T(8,128)(2,1)S(1)}, u32[]{:S(2)}, u32[]{:S(2)}) %collective-permute-start.73) | collective-permute-done | bytes 258080 | tf_op jit(solution)/shard_map/ppermute | solution.py:89
  21.2 0.5 collective-permute-start.76
  21.8 4.2 %collective-permute-done.76 = bf16[64,896]{1,0:T(8,128)(2,1)S(1)} collective-permute-done((bf16[64,896]{1,0:T(8,128)(2,1)S(1)}, bf16[64,896]{1,0:T(8,128)(2,1)S(1)}, u32[]{:S(2)}, u32[]{:S(2)}) %collective-permute-start.76) | collective-permute-done | bytes 114720 | tf_op jit(solution)/shard_map/ppermute | solution.py:89
  26.2 5.0 %shard_map.75 = (bf16[1024,3584]{1,0:T(8,128)(2,1)S(1)}, bf16[512,3584]{1,0:T(8,128)(2,1)S(1)}) custom-call(s32[2]{0:T(128)S(1)} %pad_add_fusion.at, bf16[4,256,7168]{2,1,0:T(8,128)(2,1)} %wg.5, bf16[4,256,7168]{2,1,0:T(8,128)(2,1)} %wu.7), custom_call_target="tpu_custom_call" | custom-call | tf_op jit(solution)/shard_map/pallas_call | solution.py:93
  31.2 3.8 %shard_map.77 = (bf16[512,3584]{1,0:T(8,128)(2,1)S(1)}, bf16[512,3584]{1,0:T(8,128)(2,1)S(1)}) custom-call(s32[2]{0:T(128)S(1)} %pad_add_fusion.at, bf16[4,256,7168]{2,1,0:T(8,128)(2,1)} %wg.5, bf16[4,256,7168]{2,1,0:T(8,128)(2,1)} %wu.7), custom_call_target="tpu_custom_call" | custom-call | tf_op jit(solution)/shard_map/pallas_call | solution.py:93
  35.0 3.0 %shard_map.76 = (bf16[128,3584]{1,0:T(8,128)(2,1)S(1)}, f32[1024,128]{1,0:T(8,128)S(1)}, f32[4,128]{1,0:T(4,128)S(1)}, f32[4,128]{1,0:T(4,128)S(1)}, f32[512,128...) custom-call(s32[2]{0:T(128)S(1)} %pad_add_fusion.at, ...), custom_call_target="tpu_custom_call" | custom-call | tf_op jit(solution)/shard_map/pallas_call | solution.py:93
  38.0 2.7 %shard_map.78 = (f32[1024,128]{1,0:T(8,128)S(1)}, bf16[512,3584]{1,0:T(8,128)(2,1)S(1)}) custom-call(s32[2]{0:T(128)S(1)} %pad_add_fusion.at, bf16[128,3584]{1,0:T(8,128)(2,1)S(1)} %get-tuple-element.177.x, bf16[512,3584]{1,0:T(8,128)(2,1)S(1)} %get-tuple-element.178.u_in0, bf16[512,3584]{1,0:T(8,128)(2,1)S(1)} %get-tuple-element.179.u_in1, ...), custom_call_target="tpu_custom_call" | custom-call | tf_op jit(solution)/shard_map/pallas_call | solution.py:93
  40.8 5.6 %shard_map.79 = bf16[512,256]{1,0:T(8,128)(2,1)S(1)} custom-call(s32[2]{0:T(128)S(1)} %pad_add_fusion.at, bf16[256,896]{1,0:T(8,128)(2,1)S(1)} %constant_dynamic-update-slice_fusion.11.mine, bf16[256,896]{1,0:T(8,128)(2,1)S(1)} %collective-permute-done.78.other, bf16[512,3584]{1,0:T(8,128)(2,1)S(1)} %get-tuple-element.175.g_in0, ...), custom_call_target="tpu_custom_call" | custom-call | tf_op jit(solution)/shard_map/pallas_call | solution.py:93
  46.4 25.2 %conditional.1 = (f32[128,896]{1,0:T(8,128)S(1)}) conditional(s32[]{:T(128)} %bitcast.4, (bf16[512,256]{1,0:T(8,128)(2,1)S(1)}, s32[2]{0:T(128)S(1)}, bf16[4,2048,896]{2,1,0:T(8,128)(2,1)}, f32[512,128]{1,0:T(8,128)S(1)}) %tuple.35, (bf16[512,256]{1,0:T(8,128)(2,1)S(1)}, s32[2]{0:T(128)S(1)}, ...), branch_computations={%region_0.0_spmd, %region_1.0_spmd, %region_2.0_spmd, %region_3.0_... | conditional | bytes 7340320 | solution.py:369
  46.5 1.3 %collective-permute-start.7 = (bf16[224,256]{1,0:T(8,128)(2,1)S(1)}, bf16[224,256]{1,0:T(8,128)(2,1)S(1)}, u32[]{:S(2)}, u32[]{:S(2)}) collective-permute-start(bf16[224,256]{1,0:T(8,128)(2,1)S(1)} %slice.36.refs_0_), channel_id=1, source_target_pairs={{0,4},{1,5},{2,6},{3,7},{4,0},{5,1},{6,2},{7,3},{8,12},{9,13},{10,... | collective-permute-start | bytes 344072 | tf_op jit(solution)/shard_map/cond/branch_1_fun/ppermute | solution.py:89
  47.7 0.6 collective-permute-start.12
  48.4 6.9 %collective-permute-done.7.refs_3_ = bf16[224,256]{1,0:T(8,128)(2,1)S(1)} collective-permute-done((bf16[224,256]{1,0:T(8,128)(2,1)S(1)}, bf16[224,256]{1,0:T(8,128)(2,1)S(1)}, u32[]{:S(2)}, u32[]{:S(2)}) %collective-permute-start.7) | collective-permute-done | bytes 114720 | tf_op jit(solution)/shard_map/cond/branch_1_fun/ppermute | solution.py:89
  55.2 0.3 collective-permute-start.9
  55.6 1.7 %collective-permute-start.11 = (bf16[224,256]{1,0:T(8,128)(2,1)S(1)}, bf16[224,256]{1,0:T(8,128)(2,1)S(1)}, u32[]{:S(2)}, u32[]{:S(2)}) collective-permute-start(bf16[224,256]{1,0:T(8,128)(2,1)S(1)} %slice.36.refs_0_), channel_id=1, source_target_pairs={{0,1},{1,0},{2,3},{3,2},{4,5},{5,4},{6,7},{7,6},{8,9},{9,8},{10,11... | collective-permute-start | bytes 344072 | tf_op jit(solution)/shard_map/cond/branch_1_fun/ppermute | solution.py:89
  57.3 0.3 collective-permute-start.13
  57.6 3.6 %collective-permute-done.9.refs_5_ = bf16[224,256]{1,0:T(8,128)(2,1)S(1)} collective-permute-done((bf16[224,256]{1,0:T(8,128)(2,1)S(1)}, bf16[224,256]{1,0:T(8,128)(2,1)S(1)}, u32[]{:S(2)}, u32[]{:S(2)}) %collective-permute-start.9) | collective-permute-done | bytes 114720 | tf_op jit(solution)/shard_map/cond/branch_1_fun/ppermute | solution.py:89
  61.3 4.9 %branch_1_fun.3.refs_7_ = bf16[4,1536,896]{2,1,0:T(8,128)(2,1)S(1)} custom-call(s32[2]{0:T(128)S(1)} %get-tuple-element.104.at, bf16[4,2048,896]{2,1,0:T(8,128)(2,1)} %get-tuple-element.197.wd.refs_8_), custom_call_target="tpu_custom_call" | custom-call | tf_op jit(solution)/shard_map/cond/branch_1_fun/pallas_call | solution.py:93
  66.2 3.5 %branch_1_fun.4 = (f32[128,896]{1,0:T(8,128)S(1)}, bf16[4,512,896]{2,1,0:T(8,128)(2,1)S(1)}) custom-call(s32[2]{0:T(128)S(1)} %get-tuple-element.104.at, bf16[224,256]{1,0:T(8,128)(2,1)S(1)} %slice.36.refs_0_, bf16[224,256]{1,0:T(8,128)(2,1)S(1)} %collective-permute-done.11.refs_1_, bf16[224,256]{1,0:T(8,128)(2,1)S(1)} %collective-permute-done.12.refs_2_, ...), custom_call_target="tpu_custom_call" | custom-call | tf_op jit(solution)/shard_map/cond/branch_1_fun/pallas_call | solution.py:93
  69.7 1.5 %branch_1_fun.5 = f32[128,896]{1,0:T(8,128)S(1)} custom-call(bf16[224,256]{1,0:T(8,128)(2,1)S(1)} %collective-permute-done.8.refs_0_, bf16[224,256]{1,0:T(8,128)(2,1)S(1)} %collective-permute-done.10.refs_1_, f32[512,128]{1,0:T(8,128)S(1)} %get-tuple-element.102.refs_6_.refs_2_, bf16[4,512,896]{2,1,0:T(8,128)(2,1)S(1)} %get-tuple-element.106.refs_3_, ...), custom_call_target="tpu_custom_call" | custom-call | tf_op jit(solution)/shard_map/cond/branch_1_fun/pallas_call | solution.py:93
  71.7 3.0 %collective-permute-start.79 = (bf16[32,896]{1,0:T(8,128)(2,1)S(1)}, bf16[32,896]{1,0:T(8,128)(2,1)S(1)}, u32[]{:S(2)}, u32[]{:S(2)}) collective-permute-start(bf16[32,896]{1,0:T(8,128)(2,1)S(1)} %get-tuple-element.206), channel_id=1, source_target_pairs={{0,16},{8,24},{16,0},{24,8},{1,17},{9,25},{17,1},{25,9},{2,18},{10... | collective-permute-start | bytes 172040 | tf_op jit(solution)/shard_map/ppermute | solution.py:89
  74.8 2.0 %collective-permute-done.79 = bf16[32,896]{1,0:T(8,128)(2,1)S(1)} collective-permute-done((bf16[32,896]{1,0:T(8,128)(2,1)S(1)}, bf16[32,896]{1,0:T(8,128)(2,1)S(1)}, u32[]{:S(2)}, u32[]{:S(2)}) %collective-permute-start.79) | collective-permute-done | bytes 57376 | tf_op jit(solution)/shard_map/ppermute | solution.py:89
  76.8 1.4 %collective-permute-done.81 = bf16[32,896]{1,0:T(8,128)(2,1)S(1)} collective-permute-done((bf16[32,896]{1,0:T(8,128)(2,1)S(1)}, bf16[32,896]{1,0:T(8,128)(2,1)S(1)}, u32[]{:S(2)}, u32[]{:S(2)}) %collective-permute-start.81) | collective-permute-done | bytes 57376 | tf_op jit(solution)/shard_map/ppermute | solution.py:89
  78.3 0.7 fusion.2
  (33 shorter events, 0.7 us)
Async XLA Ops:
  0.0 6.6 %collective-permute-start.70 = (bf16[32,896]{1,0:T(8,128)(2,1)}, bf16[32,896]{1,0:T(8,128)(2,1)S(1)}, u32[]{:S(2)}, u32[]{:S(2)}) collective-permute-start(bf16[32,896]{1,0:T(8,128)(2,1)} %tokens.1), channel_id=1, source_target_pairs={{0,2},{1,3},{2,0},{3,1},{4,6},{5,7},{6,4},{7,5},{8,10},{9,11},{10,... | collective-permute-start | bytes 172040 | tf_op jit(solution)/shard_map/ppermute | solution.py:89
  3.1 6.4 %collective-permute-start.71 = (bf16[32,896]{1,0:T(8,128)(2,1)}, bf16[32,896]{1,0:T(8,128)(2,1)S(1)}, u32[]{:S(2)}, u32[]{:S(2)}) collective-permute-start(bf16[32,896]{1,0:T(8,128)(2,1)} %tokens.1), channel_id=1, source_target_pairs={{0,4},{1,5},{2,6},{3,7},{4,0},{5,1},{6,2},{7,3},{8,12},{9,13},{10,... | collective-permute-start | bytes 172040 | tf_op jit(solution)/shard_map/ppermute | solution.py:89
  5.6 6.2 %collective-permute-start.72 = (bf16[32,896]{1,0:T(8,128)(2,1)}, bf16[32,896]{1,0:T(8,128)(2,1)S(1)}, u32[]{:S(2)}, u32[]{:S(2)}) collective-permute-start(bf16[32,896]{1,0:T(8,128)(2,1)} %tokens.1), channel_id=1, source_target_pairs={{0,6},{1,7},{2,4},{3,5},{4,2},{5,3},{6,0},{7,1},{8,14},{9,15},{10,... | collective-permute-start | bytes 172040 | tf_op jit(solution)/shard_map/ppermute | solution.py:89
  11.9 6.1 %collective-permute-start.75 = (bf16[128,896]{1,0:T(8,128)(2,1)S(1)}, bf16[128,896]{1,0:T(8,128)(2,1)S(1)}, u32[]{:S(2)}, u32[]{:S(2)}) collective-permute-start(bf16[128,896]{1,0:T(8,128)(2,1)S(1)} %pad_maximum_fusion), channel_id=1, source_target_pairs={{0,1},{1,0},{2,3},{3,2},{4,5},{5,4},{6,7},{7,6},{8,9},{9,8},{10,11... | collective-permute-start | bytes 688136 | tf_op jit(solution)/shard_map/ppermute | solution.py:89
  13.5 7.6 %collective-permute-start.73 = (bf16[144,896]{1,0:T(8,128)(2,1)S(1)}, bf16[144,896]{1,0:T(8,128)(2,1)S(1)}, u32[]{:S(2)}, u32[]{:S(2)}) collective-permute-start(bf16[144,896]{1,0:T(8,128)(2,1)S(1)} %get-tuple-element.217), channel_id=1, source_target_pairs={{0,16},{8,24},{16,0},{24,8},{1,17},{9,25},{17,1},{25,9},{2,18},{10... | collective-permute-start | bytes 774152 | tf_op jit(solution)/shard_map/ppermute | solution.py:89
  18.0 8.1 %collective-permute-start.77 = (bf16[64,896]{1,0:T(8,128)(2,1)S(1)}, bf16[64,896]{1,0:T(8,128)(2,1)S(1)}, u32[]{:S(2)}, u32[]{:S(2)}) collective-permute-start(bf16[64,896]{1,0:T(8,128)(2,1)S(1)} %slice.57), channel_id=1, source_target_pairs={{0,16},{8,24},{16,0},{24,8},{1,17},{9,25},{17,1},{25,9},{2,18},{10... | collective-permute-start | bytes 344072 | tf_op jit(solution)/shard_map/ppermute | solution.py:89
  21.2 4.9 %collective-permute-start.76 = (bf16[64,896]{1,0:T(8,128)(2,1)S(1)}, bf16[64,896]{1,0:T(8,128)(2,1)S(1)}, u32[]{:S(2)}, u32[]{:S(2)}) collective-permute-start(bf16[64,896]{1,0:T(8,128)(2,1)S(1)} %slice.56), channel_id=1, source_target_pairs={{0,1},{1,0},{2,3},{3,2},{4,5},{5,4},{6,7},{7,6},{8,9},{9,8},{10,11... | collective-permute-start | bytes 344072 | tf_op jit(solution)/shard_map/ppermute | solution.py:89
  21.7 13.3 %collective-permute-start.74 = (bf16[288,896]{1,0:T(8,128)(2,1)S(1)}, bf16[288,896]{1,0:T(8,128)(2,1)S(1)}, u32[]{:S(2)}, u32[]{:S(2)}) collective-permute-start(bf16[288,896]{1,0:T(8,128)(2,1)S(1)} %constant_dynamic-update-slice_fusion.5.mine), channel_id=1, source_target_pairs={{0,8},{8,0},{16,24},{24,16},{1,9},{9,1},{17,25},{25,17},{2,10},{10... | collective-permute-start | bytes 1548296 | tf_op jit(solution)/shard_map/ppermute | solution.py:89
  26.1 14.7 %collective-permute-start.78 = (bf16[256,896]{1,0:T(8,128)(2,1)S(1)}, bf16[256,896]{1,0:T(8,128)(2,1)S(1)}, u32[]{:S(2)}, u32[]{:S(2)}) collective-permute-start(bf16[256,896]{1,0:T(8,128)(2,1)S(1)} %constant_dynamic-update-slice_fusion.11.mine), channel_id=1, source_target_pairs={{0,8},{8,0},{16,24},{24,16},{1,9},{9,1},{17,25},{25,17},{2,10},{10... | collective-permute-start | bytes 1376264 | tf_op jit(solution)/shard_map/ppermute | solution.py:89
  46.5 8.8 %collective-permute-start.7 = (bf16[224,256]{1,0:T(8,128)(2,1)S(1)}, bf16[224,256]{1,0:T(8,128)(2,1)S(1)}, u32[]{:S(2)}, u32[]{:S(2)}) collective-permute-start(bf16[224,256]{1,0:T(8,128)(2,1)S(1)} %slice.36.refs_0_), channel_id=1, source_target_pairs={{0,4},{1,5},{2,6},{3,7},{4,0},{5,1},{6,2},{7,3},{8,12},{9,13},{10,... | collective-permute-start | bytes 344072 | tf_op jit(solution)/shard_map/cond/branch_1_fun/ppermute | solution.py:89
  47.7 9.5 %collective-permute-start.12 = (bf16[224,256]{1,0:T(8,128)(2,1)S(1)}, bf16[224,256]{1,0:T(8,128)(2,1)S(1)}, u32[]{:S(2)}, u32[]{:S(2)}) collective-permute-start(bf16[224,256]{1,0:T(8,128)(2,1)S(1)} %slice.36.refs_0_), channel_id=1, source_target_pairs={{0,2},{1,3},{2,0},{3,1},{4,6},{5,7},{6,4},{7,5},{8,10},{9,11},{10,... | collective-permute-start | bytes 344072 | tf_op jit(solution)/shard_map/cond/branch_1_fun/ppermute | solution.py:89
  55.2 6.0 %collective-permute-start.9 = (bf16[224,256]{1,0:T(8,128)(2,1)S(1)}, bf16[224,256]{1,0:T(8,128)(2,1)S(1)}, u32[]{:S(2)}, u32[]{:S(2)}) collective-permute-start(bf16[224,256]{1,0:T(8,128)(2,1)S(1)} %collective-permute-done.7.refs_3_), channel_id=1, source_target_pairs={{0,1},{1,0},{2,3},{3,2},{4,5},{5,4},{6,7},{7,6},{8,9},{9,8},{10,11... | collective-permute-start | bytes 344072 | tf_op jit(solution)/shard_map/cond/branch_1_fun/ppermute | solution.py:89
  55.6 10.6 %collective-permute-start.11 = (bf16[224,256]{1,0:T(8,128)(2,1)S(1)}, bf16[224,256]{1,0:T(8,128)(2,1)S(1)}, u32[]{:S(2)}, u32[]{:S(2)}) collective-permute-start(bf16[224,256]{1,0:T(8,128)(2,1)S(1)} %slice.36.refs_0_), channel_id=1, source_target_pairs={{0,1},{1,0},{2,3},{3,2},{4,5},{5,4},{6,7},{7,6},{8,9},{9,8},{10,11... | collective-permute-start | bytes 344072 | tf_op jit(solution)/shard_map/cond/branch_1_fun/ppermute | solution.py:89
  57.3 8.9 %collective-permute-start.13 = (bf16[224,256]{1,0:T(8,128)(2,1)S(1)}, bf16[224,256]{1,0:T(8,128)(2,1)S(1)}, u32[]{:S(2)}, u32[]{:S(2)}) collective-permute-start(bf16[224,256]{1,0:T(8,128)(2,1)S(1)} %collective-permute-done.12.refs_2_), channel_id=1, source_target_pairs={{0,1},{1,0},{2,3},{3,2},{4,5},{5,4},{6,7},{7,6},{8,9},{9,8},{10,11... | collective-permute-start | bytes 344072 | tf_op jit(solution)/shard_map/cond/branch_1_fun/ppermute | solution.py:89
  57.6 12.1 %collective-permute-start.8 = (bf16[224,256]{1,0:T(8,128)(2,1)S(1)}, bf16[224,256]{1,0:T(8,128)(2,1)S(1)}, u32[]{:S(2)}, u32[]{:S(2)}) collective-permute-start(bf16[224,256]{1,0:T(8,128)(2,1)S(1)} %collective-permute-done.7.refs_3_), channel_id=1, source_target_pairs={{0,2},{1,3},{2,0},{3,1},{4,6},{5,7},{6,4},{7,5},{8,10},{9,11},{10,... | collective-permute-start | bytes 344072 | tf_op jit(solution)/shard_map/cond/branch_1_fun/ppermute | solution.py:89
  61.3 8.4 %collective-permute-start.10 = (bf16[224,256]{1,0:T(8,128)(2,1)S(1)}, bf16[224,256]{1,0:T(8,128)(2,1)S(1)}, u32[]{:S(2)}, u32[]{:S(2)}) collective-permute-start(bf16[224,256]{1,0:T(8,128)(2,1)S(1)} %collective-permute-done.9.refs_5_), channel_id=1, source_target_pairs={{0,2},{1,3},{2,0},{3,1},{4,6},{5,7},{6,4},{7,5},{8,10},{9,11},{10,... | collective-permute-start | bytes 344072 | tf_op jit(solution)/shard_map/cond/branch_1_fun/ppermute | solution.py:89
  71.7 5.2 %collective-permute-start.79 = (bf16[32,896]{1,0:T(8,128)(2,1)S(1)}, bf16[32,896]{1,0:T(8,128)(2,1)S(1)}, u32[]{:S(2)}, u32[]{:S(2)}) collective-permute-start(bf16[32,896]{1,0:T(8,128)(2,1)S(1)} %get-tuple-element.206), channel_id=1, source_target_pairs={{0,16},{8,24},{16,0},{24,8},{1,17},{9,25},{17,1},{25,9},{2,18},{10... | collective-permute-start | bytes 172040 | tf_op jit(solution)/shard_map/ppermute | solution.py:89
  74.7 2.2 %collective-permute-start.80 = (bf16[32,896]{1,0:T(8,128)(2,1)S(1)}, bf16[32,896]{1,0:T(8,128)(2,1)S(1)}, u32[]{:S(2)}, u32[]{:S(2)}) collective-permute-start(bf16[32,896]{1,0:T(8,128)(2,1)S(1)} %get-tuple-element.208), channel_id=1, source_target_pairs={{0,8},{8,0},{16,24},{24,16},{1,9},{9,1},{17,25},{25,17},{2,10},{10... | collective-permute-start | bytes 172040 | tf_op jit(solution)/shard_map/ppermute | solution.py:89
  74.7 3.6 %collective-permute-start.81 = (bf16[32,896]{1,0:T(8,128)(2,1)S(1)}, bf16[32,896]{1,0:T(8,128)(2,1)S(1)}, u32[]{:S(2)}, u32[]{:S(2)}) collective-permute-start(bf16[32,896]{1,0:T(8,128)(2,1)S(1)} %get-tuple-element.207), channel_id=1, source_target_pairs={{0,24},{8,16},{16,8},{24,0},{1,25},{9,17},{17,9},{25,1},{2,26},{10... | collective-permute-start | bytes 172040 | tf_op jit(solution)/shard_map/ppermute | solution.py:89
